TPU v7x, 32 devices: a whole 2x2x4 slice. The times are simulated.
32 devices in a mesh: expert: 8 (over z, x), mp: 4 (over y, core).
Axes of the slice: x: 2, y: 2, z: 4, core: 2. Of those that a mesh axis runs over, the one named last changes fastest.
Arguments:
- tokens: bfloat16 [2048, 1024], P('expert'), may hold values from -6 to 6
- cotangent: bfloat16 [2048, 1024], P('expert'), may hold values from -6 to 6
- routes: int32 [2048, 2], P('expert'), may hold values from 0 to 7, all different within a row; in each aligned block of 256 rows (0 to 255, 256 to 511, ...) at most 96 rows name the same one
- router_weight: bfloat16 [1024, 8], replicated, may hold values from -0.1875 to 0.1875
- gate_weight: bfloat16 [8, 1024, 3584], P('expert', None, 'mp'), may hold values from -0.1875 to 0.1875
- up_weight: bfloat16 [8, 1024, 3584], P('expert', None, 'mp'), may hold values from -0.6875 to 0.6875
- down_weight: bfloat16 [8, 3584, 1024], P('expert', 'mp'), may hold values from -0.3674842 to 0.3674842
- mlp_in: float32 [3, 16], replicated, may hold values from -3.5 to 3.5
- mlp_bias: float32 [16], replicated, may hold values from -2 to 2
- mlp_out: float32 [16], replicated, may hold values from -1.5 to 1.5
Outputs:
- mixed: bfloat16 [2048, 1024], P('expert', 'mp')
- gate_update: bfloat16 [8, 1024, 3584], P('expert', None, 'mp')
- up_update: bfloat16 [8, 1024, 3584], P('expert', None, 'mp')
- down_update: bfloat16 [8, 3584, 1024], P('expert', 'mp')
- router_update: bfloat16 [1024, 8], replicated
Inputs may be any that keep to these rules, and one draw needn't show every extreme that they name: `routes`: in the rows of one index of the expert axis each expert is named at most 96 times; the two experts of a row differ.
All inputs are finite; a program needn't handle non-finite values.
Results may differ from a plain program's by a relative error of at most 0.0057.
Values may be sent and summed in bfloat16 or wider, within the bound.
A program may use at most 128 MiB of HBM per device.

v0:
```python
import functools

import jax
import jax.numpy as jnp
from jax import lax
from jax.experimental import pallas as pl
from jax.experimental.pallas import tpu as pltpu
from jax.sharding import PartitionSpec as P

EPSILON = 1e-06
CHUNK = 128
MESH = pl.DeviceIdType.MESH


def dispatch_kernel(n, groups, colw, send_ref, out_ref, loc, s1, r1, ls, lr, hs, hr, fs, fr):
    me = lax.axis_index("expert")
    col = lax.axis_index("mp")
    partner = col + 1 - 2 * lax.rem(col, 2)
    highs = groups // 2
    barrier = pltpu.get_barrier_semaphore()

    def greet(i, _):
        pl.semaphore_signal(
            barrier, inc=1, device_id=(lax.rem(me + i, n), col), device_id_type=MESH
        )
        return 0

    lax.fori_loop(1, n, greet, 0)
    pl.semaphore_signal(barrier, inc=1, device_id=(me, partner), device_id_type=MESH)
    for h in range(1, highs):
        pl.semaphore_signal(
            barrier, inc=1, device_id=(me, lax.rem(col + 2 * h, groups)), device_id_type=MESH
        )
    pl.semaphore_wait(barrier, n - 1 + 1 + highs - 1)

    def cols(c):
        return pl.ds(pl.multiple_of(c * colw, 128), colw)

    def spread(i):
        peer = lax.rem(me + i, n)
        return pltpu.make_async_remote_copy(
            src_ref=send_ref.at[:, peer],
            dst_ref=out_ref.at[:, me, :, cols(col)],
            send_sem=s1.at[i],
            recv_sem=r1.at[i],
            device_id=(peer, col),
            device_id_type=MESH,
        )

    def block(owner, i):
        return out_ref.at[:, lax.rem(me - i + n, n), :, cols(owner)]

    def to(owner, i, send, recv, target):
        ref = block(owner, i)
        return pltpu.make_async_remote_copy(
            src_ref=ref,
            dst_ref=ref,
            send_sem=send,
            recv_sem=recv,
            device_id=(me, target),
            device_id_type=MESH,
        )

    def low(i):
        return to(col, i, ls.at[i], lr.at[i], partner)

    def high(h, i):
        return to(col, i, hs.at[h - 1, i], hr.at[h - 1, i], lax.rem(col + 2 * h, groups))

    def forward(h, i):
        owner = lax.rem(col - 2 * h + 2 * groups, groups)
        return to(owner, i, fs.at[h - 1, i], fr.at[h - 1, i], partner)

    own = pltpu.make_async_copy(send_ref.at[:, me], out_ref.at[:, me, :, cols(col)], loc)
    own.start()

    def start(i, _):
        spread(i).start()
        return 0

    lax.fori_loop(1, n, start, 0)
    own.wait()

    def share(i):
        for h in range(1, highs):
            high(h, i).start()
        low(i).start()

    def relay(i):
        for h in range(1, highs):
            high(h, i).wait_recv()
            forward(h, i).start()

    share(0)

    def step(i, _):
        spread(i).wait_recv()
        share(i)
        relay(i - 1)
        return 0

    lax.fori_loop(1, n, step, 0)
    relay(n - 1)

    def finish(i, _):
        low(i).wait()
        for h in range(1, highs):
            high(h, i).wait_send()
            forward(h, i).wait()
        return 0

    def finish_spread(i, _):
        spread(i).wait_send()
        return 0

    lax.fori_loop(0, n, finish, 0)
    lax.fori_loop(1, n, finish_spread, 0)


def dispatch(send, n, groups):
    _, _, cap, colw = send.shape
    dma = pltpu.SemaphoreType.DMA
    highs = max(groups // 2 - 1, 1)
    return pl.pallas_call(
        functools.partial(dispatch_kernel, n, groups, colw),
        out_shape=jax.ShapeDtypeStruct((2, n, cap, colw * groups), send.dtype),
        in_specs=[pl.BlockSpec(memory_space=pltpu.VMEM)],
        out_specs=pl.BlockSpec(memory_space=pltpu.VMEM),
        scratch_shapes=[
            dma,
            dma((n,)),
            dma((n,)),
            dma((n,)),
            dma((n,)),
            dma((highs, n)),
            dma((highs, n)),
            dma((highs, n)),
            dma((highs, n)),
        ],
        compiler_params=pltpu.CompilerParams(collective_id=0, has_side_effects=True),
        name="dispatch",
    )(send)


def gather_sums_kernel(n, groups, x_ref, out_ref, parts, mine, ms, mr, es, er):
    me = lax.axis_index("expert")
    col = lax.axis_index("mp")
    barrier = pltpu.get_barrier_semaphore()

    def greet_mp(i, _):
        pl.semaphore_signal(
            barrier, inc=1, device_id=(me, lax.rem(col + i, groups)), device_id_type=MESH
        )
        return 0

    def greet(i, _):
        pl.semaphore_signal(
            barrier, inc=1, device_id=(lax.rem(me + i, n), col), device_id_type=MESH
        )
        return 0

    lax.fori_loop(1, groups, greet_mp, 0)
    lax.fori_loop(1, n, greet, 0)
    parts[col] = x_ref[...]
    pl.semaphore_wait(barrier, groups - 1 + n - 1)

    def across(i):
        return pltpu.make_async_remote_copy(
            src_ref=x_ref,
            dst_ref=parts.at[col],
            send_sem=ms.at[i],
            recv_sem=mr.at[i],
            device_id=(me, lax.rem(col + i, groups)),
            device_id_type=MESH,
        )

    def spread(i):
        return pltpu.make_async_remote_copy(
            src_ref=mine,
            dst_ref=out_ref.at[me],
            send_sem=es.at[i],
            recv_sem=er.at[i],
            device_id=(lax.rem(me + i, n), col),
            device_id_type=MESH,
        )

    def start_across(i, _):
        across(i).start()
        return 0

    def finish_across(i, _):
        across(i).wait()
        return 0

    def start(i, _):
        spread(i).start()
        return 0

    def finish(i, _):
        spread(i).wait()
        return 0

    lax.fori_loop(1, groups, start_across, 0)
    lax.fori_loop(1, groups, finish_across, 0)
    total = parts[0]
    for i in range(1, groups):
        total = total + parts[i]
    mine[...] = total
    out_ref[me] = total
    lax.fori_loop(1, n, start, 0)
    lax.fori_loop(1, n, finish, 0)


def gather_sums(x, n, groups):
    dma = pltpu.SemaphoreType.DMA
    return pl.pallas_call(
        functools.partial(gather_sums_kernel, n, groups),
        out_shape=jax.ShapeDtypeStruct((n,) + x.shape, x.dtype),
        in_specs=[pl.BlockSpec(memory_space=pltpu.VMEM)],
        out_specs=pl.BlockSpec(memory_space=pltpu.VMEM),
        scratch_shapes=[
            pltpu.VMEM((groups,) + x.shape, x.dtype),
            pltpu.VMEM(x.shape, x.dtype),
            dma((groups,)),
            dma((groups,)),
            dma((n,)),
            dma((n,)),
        ],
        compiler_params=pltpu.CompilerParams(collective_id=1, has_side_effects=True),
        name="gather_sums",
    )(x)


def update_kernel(units, chunk, scale, inv_ref, coef_ref, g_ref, w_ref, out_ref):
    rows, width = g_ref.shape
    strips = width // 128
    inv = inv_ref[0]

    def body(step, _):
        r = pl.ds(pl.multiple_of((step // strips) * chunk, chunk), chunk)
        c = pl.ds(pl.multiple_of(lax.rem(step, strips) * 128, 128), 128)

        def coef(i):
            return jnp.concatenate([coef_ref[i]] * (chunk // 8), axis=0)

        f0 = g_ref[r, c] * inv
        f1 = w_ref[r, c].astype(jnp.float32) * scale
        f2 = jnp.tanh(f0)
        acc = coef(5 * units)
        for j in range(units):
            y = coef(j) * f0 + coef(units + j) * f1 + coef(2 * units + j) * f2
            acc = acc + coef(4 * units + j) * jnp.maximum(y, coef(3 * units + j))
        out_ref[r, c] = acc.astype(jnp.bfloat16)
        return 0

    lax.fori_loop(0, (rows // chunk) * strips, body, 0)


def update_send_kernel(
    units, chunk, scale, n, inv_ref, coef_ref, g_ref, w_ref, part_ref, rows_ref, out_ref, total_ref, back_ref, parts, returned, outgoing, ls, ps, pr, qs, qr
):
    me = lax.axis_index("expert")
    col = lax.axis_index("mp")
    step = pl.program_id(0)

    def part(i):
        return pltpu.make_async_remote_copy(
            src_ref=parts.at[me],
            dst_ref=parts.at[me],
            send_sem=ps.at[i],
            recv_sem=pr.at[i],
            device_id=(lax.rem(me + i, n), col),
            device_id_type=MESH,
        )

    def back(i):
        peer = lax.rem(me + i, n)
        return pltpu.make_async_remote_copy(
            src_ref=outgoing.at[peer],
            dst_ref=returned.at[me],
            send_sem=qs.at[i],
            recv_sem=qr.at[i],
            device_id=(peer, col),
            device_id_type=MESH,
        )

    def own():
        return (
            pltpu.make_async_copy(part_ref, parts.at[me], ls.at[0]),
            pltpu.make_async_copy(rows_ref.at[me], returned.at[me], ls.at[1]),
            pltpu.make_async_copy(rows_ref, outgoing, ls.at[2]),
        )

    @pl.when(step == 0)
    def _():
        barrier = pltpu.get_barrier_semaphore()

        def greet(i, _):
            pl.semaphore_signal(
                barrier, inc=1, device_id=(lax.rem(me + i, n), col), device_id_type=MESH
            )
            return 0

        lax.fori_loop(1, n, greet, 0)
        for copy in own():
            copy.start()
        for copy in own():
            copy.wait()
        pl.semaphore_wait(barrier, n - 1)

        def start(i, _):
            part(i).start()
            back(i).start()
            return 0

        lax.fori_loop(1, n, start, 0)

    update_kernel(units, chunk, scale, inv_ref, coef_ref, g_ref, w_ref, out_ref)

    @pl.when(step == pl.num_programs(0) - 1)
    def _():
        def finish(i, _):
            part(i).wait()
            back(i).wait()
            return 0

        lax.fori_loop(1, n, finish, 0)
        total_ref[...] = parts[0]

        def add(i, _):
            total_ref[...] += parts[i]
            return 0

        lax.fori_loop(1, n, add, 0)
        back_ref[...] = returned[...]


def network_table(mlp_in, mlp_bias, mlp_out):
    rows = jnp.concatenate(
        [mlp_in.reshape(-1), -mlp_bias, mlp_out, jnp.sum(mlp_out * mlp_bias)[None]]
    )
    return jnp.broadcast_to(rows[:, None, None], (rows.shape[0], 8, 128))


def update(g, w, scale, rms, table, send=None):
    units = table.shape[0] // 5
    inv = (1.0 / rms).reshape(1)
    rows, width = g.shape
    chunk = CHUNK if rows % CHUNK == 0 else rows
    steps = 4 if rows % (4 * chunk) == 0 else 2 if rows % (2 * chunk) == 0 else 1
    if chunk == rows:
        chunk = 8
    block = rows // steps
    in_specs = [
        pl.BlockSpec(memory_space=pltpu.SMEM),
        pl.BlockSpec(table.shape, lambda i: (0, 0, 0)),
        pl.BlockSpec((block, width), lambda i: (i, 0)),
        pl.BlockSpec((block, width), lambda i: (i, 0)),
    ]
    out_shape = jax.ShapeDtypeStruct((rows, width), jnp.bfloat16)
    out_spec = pl.BlockSpec((block, width), lambda i: (i, 0))
    cost = pl.CostEstimate(
        flops=rows * width * 9 * units, bytes_accessed=rows * width * 8, transcendentals=rows * width
    )
    if send is None:
        return pl.pallas_call(
            functools.partial(update_kernel, units, chunk, scale),
            grid=(steps,),
            out_shape=out_shape,
            in_specs=in_specs,
            out_specs=out_spec,
            cost_estimate=cost,
            name="update",
        )(inv, table, g, w)
    part, rows_back = send
    n = rows_back.shape[0]
    dma = pltpu.SemaphoreType.DMA
    return pl.pallas_call(
        functools.partial(update_send_kernel, units, chunk, scale, n),
        grid=(steps,),
        out_shape=(
            out_shape,
            jax.ShapeDtypeStruct(part.shape, part.dtype),
            jax.ShapeDtypeStruct(rows_back.shape, rows_back.dtype),
        ),
        in_specs=in_specs + [pl.BlockSpec(memory_space=pl.ANY)] * 2,
        out_specs=(
            out_spec,
            pl.BlockSpec(part.shape, lambda i: (0, 0)),
            pl.BlockSpec(rows_back.shape, lambda i: (0, 0, 0)),
        ),
        scratch_shapes=[
            pltpu.VMEM((n,) + part.shape, part.dtype),
            pltpu.VMEM(rows_back.shape, rows_back.dtype),
            pltpu.VMEM(rows_back.shape, rows_back.dtype),
            dma((3,)), dma((n,)), dma((n,)), dma((n,)), dma((n,))],
        cost_estimate=cost,
        compiler_params=pltpu.CompilerParams(collective_id=2, has_side_effects=True),
        name="update_send",
    )(inv, table, g, w, part, rows_back)


def route_tables(routes, experts, capacity):
    chosen = (routes[:, :, None] == jnp.arange(experts, dtype=jnp.int32)[None, None, :]).astype(
        jnp.int32
    )
    flat_picks = chosen.reshape(-1, experts)
    before = jnp.cumsum(flat_picks, axis=0) - flat_picks
    places = jnp.sum(before * flat_picks, axis=1).reshape(routes.shape)
    slot_hit = (places[:, :, None] == jnp.arange(capacity, dtype=jnp.int32)[None, None, :]).astype(
        jnp.bfloat16
    )
    mover = chosen.astype(jnp.bfloat16)[:, :, :, None] * slot_hit[:, :, None, :]
    return (chosen.astype(jnp.float32), mover)


def on_device(
    tokens,
    cotangent,
    routes,
    router_weight,
    gate_weight,
    up_weight,
    down_weight,
    mlp_in,
    mlp_bias,
    mlp_out,
):
    experts = lax.axis_size("expert")
    groups = lax.axis_size("mp")
    tok_count = tokens.shape[0]
    capacity = 3 * tok_count // experts
    width = tokens.shape[1]
    col_width = width // groups
    mp = lax.axis_index("mp")
    me = lax.axis_index("expert")
    col_start = mp * col_width
    chosen, mover = route_tables(routes, experts, capacity)
    logits = jnp.dot(tokens, router_weight, preferred_element_type=jnp.float32)
    picked = jnp.sum(logits[:, None, :] * chosen, axis=2)
    sigmas = jax.nn.sigmoid(picked)
    denominator = jnp.sum(sigmas, axis=1, keepdims=True)
    gates = sigmas / denominator
    token_cols = lax.dynamic_slice_in_dim(tokens, col_start, col_width, 1)
    cot_cols = lax.dynamic_slice_in_dim(cotangent, col_start, col_width, 1)
    scaled_cot = (gates[:, :, None] * cot_cols.astype(jnp.float32)[:, None, :]).astype(
        jnp.bfloat16
    )
    send_x = jnp.einsum(
        "tkec,td->ecd", mover, token_cols, preferred_element_type=jnp.float32
    ).astype(jnp.bfloat16)
    send_dy = jnp.einsum(
        "tkec,tkd->ecd", mover, scaled_cot, preferred_element_type=jnp.float32
    ).astype(jnp.bfloat16)
    got = dispatch(jnp.stack([send_x, send_dy]), experts, groups)
    slots = experts * capacity
    rows_x = got[0].reshape(slots, width)
    rows_dy = got[1].reshape(slots, width)
    w_gate = gate_weight[0]
    w_up = up_weight[0]
    w_down = down_weight[0]
    hidden_units = w_gate.shape[1] * groups
    act_gate = jnp.dot(rows_x, w_gate, preferred_element_type=jnp.float32)
    act_up = jnp.dot(rows_x, w_up, preferred_element_type=jnp.float32)
    sigmoid_gate = jax.nn.sigmoid(act_gate)
    silu_gate = act_gate * sigmoid_gate
    hidden = (silu_gate * act_up).astype(jnp.bfloat16)
    partial_out = jnp.dot(hidden, w_down, preferred_element_type=jnp.float32).astype(jnp.bfloat16)
    grad_down = jnp.einsum("sf,sd->fd", hidden, rows_dy, preferred_element_type=jnp.float32)
    grad_hidden = jnp.einsum("sd,fd->sf", rows_dy, w_down, preferred_element_type=jnp.float32)
    d_gate = (grad_hidden * act_up * sigmoid_gate * (1.0 + act_gate * (1.0 - sigmoid_gate))).astype(
        jnp.bfloat16
    )
    d_up = (grad_hidden * silu_gate).astype(jnp.bfloat16)
    d_gate, d_up = lax.optimization_barrier((d_gate, d_up))
    inner = jnp.sum(grad_hidden * hidden.astype(jnp.float32), axis=1)
    grad_gate = jnp.einsum("sd,sf->df", rows_x, d_gate, preferred_element_type=jnp.float32)
    grad_up = jnp.einsum("sd,sf->df", rows_x, d_up, preferred_element_type=jnp.float32)

    norms = jnp.stack(
        [
            jnp.sum(grad_gate * grad_gate),
            jnp.sum(grad_up * grad_up),
            jnp.sum(grad_down * grad_down),
        ]
    )
    need = slots + 3
    lines = -(-need // 1024) * 8
    parcel = jnp.concatenate([inner, norms, jnp.zeros((lines * 128 - need,), jnp.float32)])
    parcels = gather_sums(parcel.reshape(lines, 128), experts, groups)
    parcels = parcels.reshape(experts, lines * 128)
    partial_out, parcels = lax.optimization_barrier((partial_out, parcels))
    total_out = lax.dynamic_slice_in_dim(partial_out, col_start, col_width, 1).astype(jnp.float32)
    for shift in range(1, groups):
        target = lax.rem(mp + shift, groups)
        piece = lax.dynamic_slice_in_dim(partial_out, target * col_width, col_width, 1)
        moved = lax.ppermute(piece, "mp", [(m, (m + shift) % groups) for m in range(groups)])
        total_out = total_out + moved.astype(jnp.float32)
    back_rows = total_out.astype(jnp.bfloat16).reshape(experts, capacity, col_width)

    norm_sums = jnp.sum(parcels[:, slots : slots + 3], axis=0)
    inner_own = lax.dynamic_slice(parcels, (0, me * capacity), (experts, capacity))

    total_count = experts * width * hidden_units
    rms = jnp.sqrt(norm_sums / total_count + EPSILON)
    table = network_table(mlp_in, mlp_bias, mlp_out)
    up_update = update(grad_up, w_up, width**0.5, rms[1], table)[None]
    down_update = update(grad_down, w_down, hidden_units**0.5, rms[2], table)[None]

    gated = jnp.sum(mover.astype(jnp.float32) * inner_own[None, None], axis=(2, 3))
    logit_grads = (gated - gates * jnp.sum(gated, axis=1, keepdims=True)) * (1.0 - sigmas)
    dense_grads = jnp.sum(logit_grads[:, :, None] * chosen, axis=1).astype(jnp.bfloat16)
    router_part = jnp.einsum("te,td->ed", dense_grads, tokens, preferred_element_type=jnp.float32)
    gate_update, router_grad, returned = update(
        grad_gate, w_gate, width**0.5, rms[0], table, send=(router_part, back_rows)
    )
    gate_update = gate_update[None]
    router_rms = jnp.sqrt(jnp.sum(router_grad * router_grad) / (width * experts) + EPSILON)
    router_update = update(router_grad, router_weight.T, width**0.5, router_rms, table).T

    routed = jnp.einsum("tkec,ecd->tkd", mover, returned, preferred_element_type=jnp.float32)
    mixed = (
        token_cols.astype(jnp.float32) + gates[:, 0:1] * routed[:, 0] + gates[:, 1:2] * routed[:, 1]
    ).astype(jnp.bfloat16)
    return (mixed, gate_update, up_update, down_update, router_update)


def solution(mesh):
    placed = (
        P("expert", None),
        P("expert", None),
        P("expert", None),
        P(),
        P("expert", None, "mp"),
        P("expert", None, "mp"),
        P("expert", "mp", None),
        P(),
        P(),
        P(),
    )
    return jax.shard_map(
        on_device,
        mesh=mesh,
        in_specs=placed,
        out_specs=(
            P("expert", "mp"),
            P("expert", None, "mp"),
            P("expert", None, "mp"),
            P("expert", "mp", None),
            P(),
        ),
        check_vma=False,
    )
```

profile of v0, /device:TPU:0, one launch (start us, length us, event | category | flops | bytes accessed | tf_op | source)
XLA Modules:
  0.0 175.8 jit_solution(9543878704136905592)
XLA Ops:
  0.6 0.9 copy.20
  2.5 1.1 reduce-window.6
  4.3 1.3 fusion.59
  5.5 0.7 fusion.39
  6.3 0.9 dynamic-slice_convert_fusion
  8.2 0.9 pad_maximum_fusion.send_ref
  9.1 35.3 %dispatch.1 = bf16[2,8,96,1024]{3,2,1,0:T(8,128)(2,1)} custom-call(bf16[2,8,96,256]{3,2,1,0:T(8,128)(2,1)} %pad_maximum_fusion.send_ref), custom_call_target="tpu_custom_call" | custom-call | tf_op jit(solution)/shard_map/dispatch/pallas_call | solution.py:124
  44.4 2.5 %fusion.55 = (bf16[1,8,96,1024]{3,2,1,0:T(8,128)(2,1)S(1)}, bf16[1,8,96,1024]{3,2,1,0:T(8,128)(2,1)S(1)}) fusion(bf16[2,8,96,1024]{3,2,1,0:T(8,128)(2,1)} %dispatch.1), kind=kLoop, calls=%fused_computation.86 | loop fusion | bytes 6291456 | tf_op jit(solution)/shard_map/slice | solution.py:457
  46.9 1.8 %fusion.50 = f32[768,896]{1,0:T(8,128)S(1)} fusion(bf16[768,1024]{1,0:T(8,128)(2,1)S(1)} %bitcast.103, bf16[1,1024,896]{2,1,0:T(8,128)(2,1)S(1)} %copy-done.2), kind=kOutput, calls=%fused_computation.81 | convolution fusion | flops 1409286144 | bytes 6160384 | tf_op jit(solution)/shard_map/dot_general | solution.py:464
  49.0 1.8 %fusion.52 = f32[768,896]{1,0:T(8,128)S(1)} fusion(bf16[768,1024]{1,0:T(8,128)(2,1)S(1)} %bitcast.104, bf16[1,1024,896]{2,1,0:T(8,128)(2,1)S(1)} %copy-done.4), kind=kOutput, calls=%fused_computation.83 | convolution fusion | flops 1409286144 | bytes 6160384 | tf_op jit(solution)/shard_map/dot_general | solution.py:463
  50.8 4.3 %multiply_reduce_fusion.3 = (f32[768]{0:T(1024)S(1)}, bf16[768,896]{1,0:T(8,128)(2,1)S(1)}, bf16[768,896]{1,0:T(8,128)(2,1)}, bf16[768,896]{1,0:T(8,128)(2,1)}) fusion(f32[768,896]{1,0:T(8,128)S(1)} %fusion.50, f32[768,896]{1,0:T(8,128)S(1)} %fusion.52, bf16[768,1024]{1,0:T(8,128)(2,1)S(1)} %bitcast.107, bf16[1,896,1024]{2,1,0:T(8,128)(2,1)S(1)} %copy-done.1), kind=kOutput, calls=%fused_computation.5 | convolution fusion | flops 1421671680 | bytes 13044736 | tf_op jit(solution)/shard_map/sd,fd->sf/dot_general | solution.py:470
  55.1 4.0 %multiply_reduce_fusion = (f32[]{:T(128)}, f32[896,1024]{1,0:T(8,128)}) fusion(bf16[768,896]{1,0:T(8,128)(2,1)S(1)} %get-tuple-element.22, bf16[768,1024]{1,0:T(8,128)(2,1)S(1)} %bitcast.108), kind=kOutput, calls=%fused_computation | convolution fusion | flops 1411121152 | bytes 6619140 | tf_op jit(solution)/shard_map/sf,sd->fd/dot_general | solution.py:469
  59.1 2.9 %convolution_convert_fusion = bf16[768,1024]{1,0:T(8,128)(2,1)} fusion(bf16[768,896]{1,0:T(8,128)(2,1)S(1)} %get-tuple-element.22, bf16[1,896,1024]{2,1,0:T(8,128)(2,1)S(1)} %copy-done.1), kind=kOutput, calls=%fused_computation.17 | convolution fusion | flops 1410072576 | bytes 4784128 | tf_op jit(solution)/shard_map/dot_general | solution.py:468
  62.0 5.8 %multiply_reduce_fusion.1 = (f32[]{:T(128)}, f32[1024,896]{1,0:T(8,128)}) fusion(bf16[768,1024]{1,0:T(8,128)(2,1)S(1)} %bitcast.105, bf16[768,896]{1,0:T(8,128)(2,1)} %get-tuple-element.13), kind=kOutput, calls=%fused_computation.1 | convolution fusion | flops 1411121152 | bytes 6619140 | tf_op jit(solution)/shard_map/sd,sf->df/dot_general | solution.py:478
  67.8 5.8 %multiply_reduce_fusion.2 = (f32[]{:T(128)}, f32[1024,896]{1,0:T(8,128)}) fusion(bf16[768,1024]{1,0:T(8,128)(2,1)} %bitcast.106, bf16[768,896]{1,0:T(8,128)(2,1)S(1)} %copy-done.11), kind=kOutput, calls=%fused_computation.2 | convolution fusion | flops 1411121152 | bytes 6619140 | tf_op jit(solution)/shard_map/sd,sf->df/dot_general | solution.py:477
  73.6 2.5 %concatenate.6 = f32[1024]{0:T(1024)} concatenate(f32[768]{0:T(1024)S(1)} %get-tuple-element.21, f32[1]{0:T(128)} %bitcast.14, f32[1]{0:T(128)} %bitcast.15, f32[1]{0:T(128)} %bitcast.16, f32[253]{0:T(256)S(1)} %broadcast_in_dim.12), dimensions={0} | concatenate | bytes 8192 | tf_op jit(solution)/shard_map/concatenate | solution.py:489
  76.1 14.1 %gather_sums.1 = f32[8,8,128]{2,1,0:T(8,128)} custom-call(f32[8,128]{1,0:T(8,128)} %bitcast.114), custom_call_target="tpu_custom_call" | custom-call | tf_op jit(solution)/shard_map/gather_sums/pallas_call | solution.py:216
  90.3 0.8 copy.27
  91.1 0.9 constant_dynamic-slice_fusion.2
  92.0 0.9 collective-permute-start.1
  92.9 1.5 collective-permute-start.2
  98.9 0.9 broadcast_in_dim.14.coef_ref
  99.8 21.6 %update.4 = bf16[896,1024]{1,0:T(8,128)(2,1)} custom-call(f32[1]{0:T(128)S(6)} %div.51.inv_ref, f32[81,8,128]{2,1,0:T(8,128)} %broadcast_in_dim.14.coef_ref, f32[896,1024]{1,0:T(8,128)} %get-tuple-element.42.g_ref, bf16[896,1024]{1,0:T(8,128)(2,1)} %bitcast.96), custom_call_target="tpu_custom_call" | custom-call | flops 132120576 | bytes 7340032 | tf_op jit(solution)/shard_map/update/pallas_call | solution.py:366
  121.4 20.1 %update.3 = bf16[1024,896]{1,0:T(8,128)(2,1)} custom-call(f32[1]{0:T(128)S(6)} %div.50.inv_ref, f32[81,8,128]{2,1,0:T(8,128)} %broadcast_in_dim.14.coef_ref, f32[1024,896]{1,0:T(8,128)} %get-tuple-element.40.g_ref, bf16[1024,896]{1,0:T(8,128)(2,1)} %bitcast.97), custom_call_target="tpu_custom_call" | custom-call | flops 132120576 | bytes 7340032 | tf_op jit(solution)/shard_map/update/pallas_call | solution.py:366
  141.5 0.8 fusion.60.part_ref
  142.3 2.2 %add_convert_fusion = bf16[768,256]{1,0:T(8,128)(2,1)} fusion(bf16[768,256]{1,0:T(8,128)(2,1)} %collective-permute-done.2, bf16[768,256]{1,0:T(8,128)(2,1)} %collective-permute-done.1, bf16[768,256]{1,0:T(8,128)(2,1)} %collective-permute-done, bf16[768,1024]{1,0:T(8,128)(2,1)S(1)} %copy-done.5, s32[]{:T(128)S(6)} %select_n.17), kind=kLoop, calls=%fused_computation.25 | loop fusion | flops 1572864 | bytes 1966084 | tf_op jit(solution)/shard_map/convert_element_type | solution.py:499
  144.4 23.8 %update_send.1 = (bf16[1024,896]{1,0:T(8,128)(2,1)}, f32[8,1024]{1,0:T(8,128)}, bf16[8,96,256]{2,1,0:T(8,128)(2,1)}) custom-call(f32[1]{0:T(128)S(6)} %div.49.inv_ref, f32[81,8,128]{2,1,0:T(8,128)} %broadcast_in_dim.14.coef_ref, f32[1024,896]{1,0:T(8,128)} %get-tuple-element.38.g_ref, bf16[1024,896]{1,0:T(8,128)(2,1)} %bitcast.101, ...), custom_call_target="tpu_custom_call" | custom-call | flops 132120576 | bytes 7340032 | tf_op jit(solution)/shard_map/update_send/pallas_call | solution.py:378
  168.3 1.5 multiply_reduce_fusion.4
  170.5 1.4 fusion.13
  171.9 1.9 %update.5 = bf16[8,1024]{1,0:T(8,128)(2,1)} custom-call(f32[1]{0:T(128)} %bitcast.29.inv_ref, f32[81,8,128]{2,1,0:T(8,128)} %broadcast_in_dim.14.coef_ref, f32[8,1024]{1,0:T(8,128)} %get-tuple-element.18.g_ref, bf16[8,1024]{1,0:T(8,128)(2,1)} %bitcast.110), custom_call_target="tpu_custom_call" | custom-call | flops 1179648 | bytes 65536 | tf_op jit(solution)/shard_map/update/pallas_call | solution.py:366
  173.8 0.8 fusion.29
  174.6 1.2 copy.29
  (56 shorter events, 5.3 us)
Async XLA Ops:
  0.6 6.8 %copy-start = (bf16[256,1024]{1,0:T(8,128)(2,1)S(1)}, bf16[256,1024]{1,0:T(8,128)(2,1)}, u32[]{:S(2)}) copy-start(bf16[256,1024]{1,0:T(8,128)(2,1)} %param.10) | copy-start | bytes 1572868
  44.4 2.5 %copy-start.2 = (bf16[1,1024,896]{2,1,0:T(8,128)(2,1)S(1)}, bf16[1,1024,896]{2,1,0:T(8,128)(2,1)}, u32[]{:S(2)}) copy-start(bf16[1,1024,896]{2,1,0:T(8,128)(2,1)} %param.15) | copy-start | bytes 5505028
  46.9 15.1 %copy-start.6 = (bf16[1,8,96,1024]{3,2,1,0:T(8,128)(2,1)}, bf16[1,8,96,1024]{3,2,1,0:T(8,128)(2,1)S(1)}, u32[]{:S(2)}) copy-start(bf16[1,8,96,1024]{3,2,1,0:T(8,128)(2,1)S(1)} %get-tuple-element.25) | copy-start | bytes 4718596
  46.9 2.1 %copy-start.4 = (bf16[1,1024,896]{2,1,0:T(8,128)(2,1)S(1)}, bf16[1,1024,896]{2,1,0:T(8,128)(2,1)}, u32[]{:S(2)}) copy-start(bf16[1,1024,896]{2,1,0:T(8,128)(2,1)} %param.14) | copy-start | bytes 5505028
  49.0 1.8 %copy-start.1 = (bf16[1,896,1024]{2,1,0:T(8,128)(2,1)S(1)}, bf16[1,896,1024]{2,1,0:T(8,128)(2,1)}, u32[]{:S(2)}) copy-start(bf16[1,896,1024]{2,1,0:T(8,128)(2,1)} %param.16) | copy-start | bytes 5505028
  62.0 5.8 %copy-start.11 = (bf16[768,896]{1,0:T(8,128)(2,1)S(1)}, bf16[768,896]{1,0:T(8,128)(2,1)}, u32[]{:S(2)}) copy-start(bf16[768,896]{1,0:T(8,128)(2,1)} %get-tuple-element.12) | copy-start | bytes 4128772
  67.8 23.2 %copy-start.5 = (bf16[768,1024]{1,0:T(8,128)(2,1)S(1)}, bf16[768,1024]{1,0:T(8,128)(2,1)}, u32[]{:S(2)}) copy-start(bf16[768,1024]{1,0:T(8,128)(2,1)} %convolution_convert_fusion) | copy-start | bytes 4718596
  73.6 21.8 %copy-start.8 = (f32[3,16]{1,0:T(4,128)S(1)}, f32[3,16]{1,0:T(4,128)}, u32[]{:S(2)}) copy-start(f32[3,16]{1,0:T(4,128)} %param.17) | copy-start | bytes 580
  73.6 21.9 %copy-start.9 = (f32[16]{0:T(128)S(1)}, f32[16]{0:T(128)}, u32[]{:S(2)}) copy-start(f32[16]{0:T(128)} %param.19) | copy-start | bytes 196
  73.6 21.9 %copy-start.10 = (f32[16]{0:T(128)S(1)}, f32[16]{0:T(128)}, u32[]{:S(2)}) copy-start(f32[16]{0:T(128)} %param.18) | copy-start | bytes 196
  92.0 50.3 %collective-permute-start = (bf16[768,256]{1,0:T(8,128)(2,1)}, bf16[768,256]{1,0:T(8,128)(2,1)}, u32[]{:S(2)}, u32[]{:S(2)}) collective-permute-start(bf16[768,256]{1,0:T(8,128)(2,1)} %get-tuple-element.27), channel_id=1, source_target_pairs={{0,1},{1,2},{2,3},{3,0},{4,5},{5,6},{6,7},{7,4},{8,9},{9,10},{10,1... | collective-permute-start | bytes 1179656 | tf_op jit(solution)/shard_map/ppermute | solution.py:497
  92.0 50.3 %collective-permute-start.1 = (bf16[768,256]{1,0:T(8,128)(2,1)S(1)}, bf16[768,256]{1,0:T(8,128)(2,1)}, u32[]{:S(2)}, u32[]{:S(2)}) collective-permute-start(bf16[768,256]{1,0:T(8,128)(2,1)S(1)} %get-tuple-element.29), channel_id=1, source_target_pairs={{0,2},{1,3},{2,0},{3,1},{4,6},{5,7},{6,4},{7,5},{8,10},{9,11},{10,... | collective-permute-start | bytes 1179656 | tf_op jit(solution)/shard_map/ppermute | solution.py:497
  92.9 49.4 %collective-permute-start.2 = (bf16[768,256]{1,0:T(8,128)(2,1)S(1)}, bf16[768,256]{1,0:T(8,128)(2,1)}, u32[]{:S(2)}, u32[]{:S(2)}) collective-permute-start(bf16[768,256]{1,0:T(8,128)(2,1)S(1)} %get-tuple-element.28), channel_id=1, source_target_pairs={{0,3},{1,0},{2,1},{3,2},{4,7},{5,4},{6,5},{7,6},{8,11},{9,8},{10,9... | collective-permute-start | bytes 1179656 | tf_op jit(solution)/shard_map/ppermute | solution.py:497
  121.4 20.1 %copy-start.7 = (s32[256,2]{0,1:T(2,128)S(1)}, s32[256,2]{0,1:T(2,128)}, u32[]{:S(2)}) copy-start(s32[256,2]{0,1:T(2,128)} %param.12) | copy-start | bytes 6148
  168.3 6.3 %copy-start.3 = (bf16[1024,896]{1,0:T(8,128)(2,1)S(1)}, bf16[1024,896]{1,0:T(8,128)(2,1)}, u32[]{:S(2)}) copy-start(bf16[1024,896]{1,0:T(8,128)(2,1)} %get-tuple-element.17) | copy-start | bytes 5505028
where the time goes:
time: 176 us
  Pallas kernels  117 us (66%)
  matrix products  30.6 us (17%)
  local copies, waits for them, and re-layouts  11.4 us (6%)
  other arithmetic  11 us (6%)
  between operations  3.63 us (2%)
  starting transfers between devices  2.35 us (1%)
    pallas_call x3, Pallas kernels, update(): pl.pallas_call(functools.partial(update_kernel, units, chunk, scale), gri...  43.5 us
    pallas_call x1, Pallas kernels, dispatch(): pl.pallas_call(functools.partial(dispatch_kernel, n, groups, colw), out_s...  35.3 us
    pallas_call x1, Pallas kernels, update(): pl.pallas_call(functools.partial(update_send_kernel, units, chunk, scale,...  23.8 us
    pallas_call x1, Pallas kernels, gather_sums(): pl.pallas_call(functools.partial(gather_sums_kernel, n, groups), out_shap...  14.1 us
    dot_general x1, matrix products, on_device(): jnp.einsum('sd,sf->df', rows_x, d_up, preferred_element_type=jnp.float32)  5.79 us
    dot_general x1, matrix products, on_device(): jnp.einsum('sd,sf->df', rows_x, d_gate, preferred_element_type=jnp.float32)  5.78 us
    dot_general x1, matrix products, on_device(): jnp.einsum('sd,fd->sf', rows_dy, w_down, preferred_element_type=jnp.float32)  4.25 us
    dot_general x1, matrix products, on_device(): jnp.einsum('sf,sd->fd', hidden, rows_dy, preferred_element_type=jnp.float32)  4.04 us
  transfers between devices with their start and end apart: 3, of which 0 were waited for; matrix products, arithmetic and copies ran while one was open for 2% of the time, Pallas kernels for 24%

commit v1 on v0

v1 whole, which is shorter than its diff:
```python
import functools

import jax
import jax.numpy as jnp
from jax import lax
from jax.experimental import pallas as pl
from jax.experimental.pallas import tpu as pltpu
from jax.sharding import PartitionSpec as P

EPSILON = 1e-06
LANES = 128
CHUNK = 128
MESH = pl.DeviceIdType.MESH
F32 = jnp.float32
BF16 = jnp.bfloat16


def lane(i, size=LANES):
    return pl.ds(pl.multiple_of(i * size, LANES), size)


def dot(a, b):
    return jnp.dot(a, b, preferred_element_type=F32)


def dot_nt(a, b):
    return lax.dot_general(a, b, (((1,), (1,)), ((), ())), preferred_element_type=F32)


def dot_tn(a, b):
    return lax.dot_general(a, b, (((0,), (0,)), ((), ())), preferred_element_type=F32)


def squares(x):
    return jnp.sum((x * x).reshape(-1, 8, LANES), axis=0)


def every(lo, hi, body):
    def step(i, _):
        body(i)
        return 0

    lax.fori_loop(lo, hi, step, 0)


def fill_table(units, table, mlp_in, mlp_bias, mlp_out):
    total = jnp.zeros((8, LANES), F32)
    for j in range(units):
        bias = jnp.full((8, LANES), mlp_bias[j], F32)
        out = jnp.full((8, LANES), mlp_out[j], F32)
        for k in range(3):
            table[k * units + j] = jnp.full((8, LANES), mlp_in[k, j], F32)
        table[3 * units + j] = -bias
        table[4 * units + j] = out
        total = total + out * bias
    table[5 * units] = total


def network(units, table, f0, f1):
    rows = f0.shape[0]

    def coef(i):
        return jnp.concatenate([table[i]] * (rows // 8), axis=0)

    f2 = jnp.tanh(f0)
    acc = coef(5 * units)
    for j in range(units):
        y = coef(j) * f0 + coef(units + j) * f1 + coef(2 * units + j) * f2
        acc = acc + coef(4 * units + j) * jnp.maximum(y, coef(3 * units + j))
    return acc.astype(BF16)


def inverse_rms(tile, count):
    total = jnp.sum(jnp.sum(tile, axis=0, keepdims=True), axis=1, keepdims=True)
    return jnp.broadcast_to(1.0 / jnp.sqrt(total / count + EPSILON), (8, LANES))


def tall(tile, rows):
    return jnp.concatenate([tile] * (rows // 8), axis=0)


def to_row(column):
    size = column.shape[0]
    r = lax.broadcasted_iota(jnp.int32, (size, LANES), 0)
    c = lax.broadcasted_iota(jnp.int32, (size, LANES), 1)
    return jnp.sum(jnp.where(r == c, column, 0.0), axis=0, keepdims=True)


def to_column(row, size):
    r = lax.broadcasted_iota(jnp.int32, (size, row.shape[1]), 0)
    c = lax.broadcasted_iota(jnp.int32, (size, row.shape[1]), 1)
    return jnp.sum(jnp.where(r == c, row, 0.0), axis=1, keepdims=True)


def flip(a, i, n):
    out, bit = 0, 1
    while bit < n:
        out = out + bit * lax.rem(a // bit + i // bit, 2)
        bit *= 2
    return out


def step_kernel(
    n, groups, cap, units, total_count,
    tokens, cot, routes, router, gate_hbm, up_hbm, down_hbm, mlp_in, mlp_bias, mlp_out,
    mixed_ref, down_out, router_out, inv_out, gate_grad, up_grad,
    m0, m1, gates, sx, sdy, rx, rdy, vg, vu, vd, hid, hid_t, rx_t, silu, slope, dcat, inner,
    gd, gg, gu, part, prec, psum, hrec, back, ret, parcel, pmp, psend, pex, norms, nmp, nsend, nex,
    rpart, rex, rsum, rmp, dout, table, inv_down, squared,
    wsem, own, osem, xsem, xhigh, ysem, yhigh, lowsem, highsem, retsem, psem, pesem, nsem, nesem, rsem, rmsem,
):
    me = lax.axis_index("expert")
    col = lax.axis_index("mp")
    parity = lax.rem(col, 2)
    pair = col // 2
    partner = col + 1 - 2 * parity
    highs = groups // 2
    toks, width = tokens.shape
    colw = width // groups
    slots = n * cap
    hidden = vg.shape[1]
    tiles = hidden // LANES
    cols = lane(col, colw)
    power = n & (n - 1) == 0

    def peer_to(i):
        return flip(me, i, n) if power else lax.rem(me + i, n)

    def peer_from(i):
        return flip(me, i, n) if power else lax.rem(me - i + n, n)

    def remote(src, dst, send, recv, expert, mp):
        return pltpu.make_async_remote_copy(
            src_ref=src, dst_ref=dst, send_sem=send, recv_sem=recv,
            device_id=(expert, mp), device_id_type=MESH,
        )

    def rows(e):
        return pl.ds(pl.multiple_of(e * cap, 16), cap)

    barrier = pltpu.get_barrier_semaphore()

    def greet(i):
        pl.semaphore_signal(barrier, inc=1, device_id=(lax.rem(me + i, n), col), device_id_type=MESH)

    def greet_mp(i):
        pl.semaphore_signal(barrier, inc=1, device_id=(me, lax.rem(col + i, groups)), device_id_type=MESH)

    every(1, n, greet)
    every(1, groups, greet_mp)

    loads = [
        pltpu.make_async_copy(gate_hbm, vg, wsem.at[0]),
        pltpu.make_async_copy(up_hbm, vu, wsem.at[1]),
        pltpu.make_async_copy(down_hbm, vd, wsem.at[2]),
    ]
    for load in loads:
        load.start()

    r0, r1 = routes[0:1, :], routes[1:2, :]
    rank = max(n, 16)
    ids = lax.broadcasted_iota(jnp.int32, (rank, toks), 0)
    picks = jnp.where((ids == r0) | (ids == r1), 1.0, 0.0)
    earlier = jnp.where(
        lax.broadcasted_iota(jnp.int32, (toks, toks), 0) < lax.broadcasted_iota(jnp.int32, (toks, toks), 1), 1.0, 0.0
    )
    before = dot(picks.astype(BF16), earlier.astype(BF16)).astype(jnp.int32)
    place = lax.broadcasted_iota(jnp.int32, (cap, toks), 0)
    for e in range(n):
        hit = place == before[e : e + 1, :]
        m0[e * cap : (e + 1) * cap, :] = jnp.where(hit & (r0 == e), 1.0, 0.0).astype(BF16)
        m1[e * cap : (e + 1) * cap, :] = jnp.where(hit & (r1 == e), 1.0, 0.0).astype(BF16)
    both = m0[...] + m1[...]
    sx[...] = dot(both, tokens[:, cols]).astype(BF16)

    def exchange(send, out, sem, high):
        def spread(i):
            peer = peer_to(i)
            return remote(send.at[rows(peer)], out.at[rows(me), cols], sem.at[0, i], sem.at[1, i], peer, col)

        def block(owner, i, send_sem, recv_sem, target):
            ref = out.at[rows(peer_from(i)), lane(owner, colw)]
            return remote(ref, ref, send_sem, recv_sem, me, target)

        def low(i):
            return block(col, i, sem.at[2, i], sem.at[3, i], partner)

        def far(h, i):
            return block(col, i, high.at[0, h - 1, i], high.at[1, h - 1, i], lax.rem(col + 2 * h, groups))

        def forward(h, i):
            owner = lax.rem(col - 2 * h + 2 * groups, groups)
            return block(owner, i, high.at[2, h - 1, i], high.at[3, h - 1, i], partner)

        def share(i):
            for h in range(1, highs):
                far(h, i).start()
            low(i).start()

        def relay(i):
            for h in range(1, highs):
                far(h, i).wait_recv()
                forward(h, i).start()

        def step(i):
            @pl.when((i > 0) & (i < n))
            def _():
                spread(i).wait_recv()

            @pl.when(i < n)
            def _():
                share(i)

            @pl.when(i > 0)
            def _():
                relay(i - 1)

        def arrived(i):
            low(i).wait_recv()
            for h in range(1, highs):
                forward(h, i).wait_recv()

        def sent(i):
            low(i).wait_send()
            for h in range(1, highs):
                far(h, i).wait_send()
                forward(h, i).wait_send()

        return spread, step, arrived, sent

    spread_x, step_x, arrived_x, sent_x = exchange(sx, rx, xsem, xhigh)
    spread_y, step_y, arrived_y, sent_y = exchange(sdy, rdy, ysem, yhigh)

    pl.semaphore_wait(barrier, n - 1 + groups - 1)
    every(1, n, lambda i: spread_x(i).start())
    own_x = pltpu.make_async_copy(sx.at[rows(me)], rx.at[rows(me), cols], own.at[0])
    own_x.start()

    logits = dot_nt(router[...], tokens[...])
    kinds = lax.broadcasted_iota(jnp.int32, (n, toks), 0)
    sigma0 = jax.nn.sigmoid(jnp.sum(jnp.where(kinds == r0, logits, 0.0), axis=0, keepdims=True))
    sigma1 = jax.nn.sigmoid(jnp.sum(jnp.where(kinds == r1, logits, 0.0), axis=0, keepdims=True))
    gates[0:1, :] = sigma0 / (sigma0 + sigma1)
    gates[1:2, :] = sigma1 / (sigma0 + sigma1)
    gates[2:3, :] = 1.0 - sigma0
    gates[3:4, :] = 1.0 - sigma1
    weight = jnp.sum(
        m0[...].astype(F32) * gates[0:1, :] + m1[...].astype(F32) * gates[1:2, :], axis=1, keepdims=True
    )
    sdy[...] = (weight * dot(both, cot[:, cols])).astype(BF16)
    own_x.wait()
    every(1, n, lambda i: spread_y(i).start())
    own_y = pltpu.make_async_copy(sdy.at[rows(me)], rdy.at[rows(me), cols], own.at[1])
    own_y.start()
    fill_table(units, table, mlp_in, mlp_bias, mlp_out)

    every(0, n + 1, step_x)
    every(0, n, arrived_x)
    own_y.wait()
    for load in loads:
        load.wait()

    def forward_tile(j):
        every(j * (n + 1) // tiles, (j + 1) * (n + 1) // tiles, step_y)
        c = lane(j)
        act = dot(rx[...], jnp.concatenate([vg[:, c], vu[:, c]], axis=1))
        act_gate, act_up = act[:, :LANES], act[:, LANES:]
        s = jax.nn.sigmoid(act_gate)
        silu_gate = act_gate * s
        h = silu_gate * act_up
        silu[:, c] = silu_gate
        slope[:, c] = act_up * s * (1.0 + act_gate * (1.0 - s))
        hid[:, c] = h.astype(BF16)
        hid_t[lane(j), :] = h.T.astype(BF16)

    every(0, tiles, forward_tile)

    def turn(j):
        rx_t[lane(j), :] = rx[:, lane(j)].astype(F32).T.astype(BF16)

    every(0, width // LANES, turn)

    def partial(m):
        part[m] = dot(hid[...], vd[:, lane(m, colw)]).astype(BF16)

    every(0, groups, partial)

    def give(q):
        return remote(part.at[2 * q + 1 - parity], prec.at[q], lowsem.at[0, q], lowsem.at[1, q], me, partner)

    every(0, highs, lambda q: give(q).start())
    every(0, n, arrived_y)

    inner[...] = jnp.zeros_like(inner)

    def back_tile(start, size):
        r = pl.ds(pl.multiple_of(start, LANES), size)
        gh = dot_nt(rdy[...], vd[r, :])
        for q in range(size // LANES):
            c = pl.ds(pl.multiple_of(start + q * LANES, LANES), LANES)
            piece = gh[:, q * LANES : (q + 1) * LANES]
            d = pl.multiple_of(2 * (start + q * LANES), LANES)
            dcat[:, pl.ds(d, LANES)] = (piece * slope[:, c]).astype(BF16)
            dcat[:, pl.ds(pl.multiple_of(d + LANES, LANES), LANES)] = (piece * silu[:, c]).astype(BF16)
            inner[...] += piece * hid[:, c].astype(F32)

    every(0, hidden // (2 * LANES), lambda j: back_tile(j * 2 * LANES, 2 * LANES))
    if hidden % (2 * LANES):
        back_tile(hidden - LANES, LANES)

    squared[...] = jnp.zeros_like(squared)

    def down_tile(m):
        c = lane(m, 2 * LANES)
        g = dot(hid_t[...], rdy[:, c])
        gd[:, c] = g
        squared[0] += squares(g[:, :LANES]) + squares(g[:, LANES:])

    every(0, width // (2 * LANES), down_tile)

    for e in range(n):
        parcel[e : e + 1, :] = to_row(jnp.sum(inner[e * cap : (e + 1) * cap, :], axis=1, keepdims=True))
    parcel[n : n + 8, :] = squared[0]

    def across(src, dst, sem, i):
        return remote(src, dst.at[col], sem.at[0, i], sem.at[1, i], me, lax.rem(col + i, groups))

    def around(src, dst, sem, i):
        return remote(src, dst.at[me], sem.at[0, i], sem.at[1, i], peer_to(i), col)

    every(1, groups, lambda i: across(parcel, pmp, psem, i).start())
    pmp[col] = parcel[...]

    def total_of(ref, count):
        acc = ref[0]
        for i in range(1, count):
            acc = acc + ref[i]
        return acc

    every(0, highs, lambda q: give(q).wait_recv())

    def lend(h):
        q = lax.rem(pair + h, highs)
        return remote(psum.at[q], hrec.at[pair], highsem.at[0, h], highsem.at[1, h], me, 2 * q + parity)

    def lend_all(h):
        q = lax.rem(pair + h, highs)
        psum[q] = (part[2 * q + parity].astype(F32) + prec[q].astype(F32)).astype(BF16)
        lend(h).start()

    every(1, highs, lend_all)

    def grad_tile(j):
        g = dot(rx_t[...], dcat[:, lane(j, 2 * LANES)])
        c = lane(j)
        gg[:, c] = g[:, :LANES]
        gu[:, c] = g[:, LANES:]
        squared[1] += squares(g[:, :LANES])
        squared[2] += squares(g[:, LANES:])

    half = tiles // 2
    every(0, half, grad_tile)
    every(1, groups, lambda i: across(parcel, pmp, psem, i).wait_recv())
    psend[...] = total_of(pmp, groups)
    every(1, n, lambda i: around(psend, pex, pesem, i).start())
    pex[me] = psend[...]
    every(half, tiles, grad_tile)
    puts = [
        pltpu.make_async_copy(gg, gate_grad, osem.at[0]),
        pltpu.make_async_copy(gu, up_grad, osem.at[1]),
    ]
    for put in puts:
        put.start()
    norms[0:8, :] = squared[1]
    norms[8:16, :] = squared[2]
    every(1, groups, lambda i: across(norms, nmp, nsem, i).start())
    nmp[col] = norms[...]
    every(1, n, lambda i: around(psend, pex, pesem, i).wait_recv())
    down_norm = pex[0, n : n + 8, :]
    for e in range(1, n):
        down_norm = down_norm + pex[e, n : n + 8, :]
    inv_down[...] = inverse_rms(down_norm, total_count)

    strips = width // LANES
    bands = hidden // CHUNK
    down_scale = float((hidden * groups) ** 0.5)

    def update_band(lo, hi):
        def body(step):
            r = pl.ds(pl.multiple_of((step // strips) * CHUNK, CHUNK), CHUNK)
            c = lane(lax.rem(step, strips))
            f0 = gd[r, c] * tall(inv_down[...], CHUNK)
            dout[r, c] = network(units, table, f0, vd[r, c].astype(F32) * down_scale)

        every(lo * strips, hi * strips, body)

    marks = [i * bands // 7 for i in range(8)]
    update_band(marks[0], marks[1])

    every(1, groups, lambda i: across(norms, nmp, nsem, i).wait_recv())
    nsend[...] = total_of(nmp, groups)
    every(1, n, lambda i: around(nsend, nex, nesem, i).start())
    nex[me] = nsend[...]

    g0, g1 = gates[0:1, :], gates[1:2, :]
    gated0 = jnp.zeros((1, toks), F32)
    gated1 = jnp.zeros((1, toks), F32)
    for e in range(n):
        column = to_column(pex[e, pl.ds(me, 1), :], cap)
        gated0 = gated0 + jnp.sum(column * m0[e * cap : (e + 1) * cap, :].astype(F32), axis=0, keepdims=True)
        gated1 = gated1 + jnp.sum(column * m1[e * cap : (e + 1) * cap, :].astype(F32), axis=0, keepdims=True)
    both_gated = gated0 + gated1
    logit0 = (gated0 - g0 * both_gated) * gates[2:3, :]
    logit1 = (gated1 - g1 * both_gated) * gates[3:4, :]
    dense = jnp.where(ids == r0, logit0, 0.0) + jnp.where(ids == r1, logit1, 0.0)
    rpart[...] = dot(dense.astype(BF16), tokens[:, cols])[:n]
    every(1, n, lambda i: around(rpart, rex, rsem, i).start())
    rex[me] = rpart[...]

    update_band(marks[1], marks[3])

    every(1, highs, lambda h: lend(h).wait_recv())
    summed = part[col].astype(F32) + prec[pair].astype(F32)
    for h in range(1, highs):
        summed = summed + hrec[lax.rem(pair + h, highs)].astype(F32)
    back[...] = summed.astype(BF16)

    def bring(i):
        peer = peer_to(i)
        return remote(back.at[rows(peer)], ret.at[rows(me)], retsem.at[0, i], retsem.at[1, i], peer, col)

    every(1, n, lambda i: bring(i).start())
    own_r = pltpu.make_async_copy(back.at[rows(me)], ret.at[rows(me)], own.at[2])
    own_r.start()

    update_band(marks[3], marks[4])
    every(1, n, lambda i: around(rpart, rex, rsem, i).wait_recv())
    rsum[...] = total_of(rex, n)
    every(1, groups, lambda i: across(rsum, rmp, rmsem, i).start())
    rmp[col] = rsum[...]

    update_band(marks[4], marks[5])
    every(1, n, lambda i: around(nsend, nex, nesem, i).wait_recv())
    both_norms = total_of(nex, n)
    inv_out[0] = inverse_rms(both_norms[0:8, :], total_count)
    inv_out[1] = inverse_rms(both_norms[8:16, :], total_count)

    update_band(marks[5], marks[6])
    every(1, groups, lambda i: across(rsum, rmp, rmsem, i).wait_recv())
    router_norm = jnp.zeros((8, LANES), F32)
    for m in range(groups):
        for s in range(colw // LANES):
            router_norm = router_norm + squares(rmp[m, :, s * LANES : (s + 1) * LANES])
    router_inv = inverse_rms(router_norm, float(n * width))
    for m in range(groups):
        for s in range(colw // LANES):
            c = slice(m * colw + s * LANES, m * colw + (s + 1) * LANES)
            f0 = rmp[m, :, s * LANES : (s + 1) * LANES] * tall(router_inv, n)
            router_out[:, c] = network(units, table, f0, router[:, c].astype(F32) * float(width**0.5))

    update_band(marks[6], marks[7])
    puts.append(pltpu.make_async_copy(dout, down_out, osem.at[2]))
    puts[-1].start()

    own_r.wait()
    every(1, n, lambda i: bring(i).wait_recv())
    mixed = tokens[:, cols].astype(F32)
    mixed = mixed + to_column(g0, toks) * dot_tn(m0[...], ret[...])
    mixed = mixed + to_column(g1, toks) * dot_tn(m1[...], ret[...])
    mixed_ref[...] = mixed.astype(BF16)

    def finish(i):
        spread_x(i).wait_send()
        spread_y(i).wait_send()
        around(psend, pex, pesem, i).wait_send()
        around(nsend, nex, nesem, i).wait_send()
        around(rpart, rex, rsem, i).wait_send()
        bring(i).wait_send()

    def finish_mp(i):
        across(parcel, pmp, psem, i).wait_send()
        across(norms, nmp, nsem, i).wait_send()
        across(rsum, rmp, rmsem, i).wait_send()

    every(1, n, finish)
    every(1, groups, finish_mp)
    every(0, n, sent_x)
    every(0, n, sent_y)
    every(0, highs, lambda q: give(q).wait_send())
    every(1, highs, lambda h: lend(h).wait_send())
    for put in puts:
        put.wait()


def fused_step(tokens, cot, routes, router, w_gate, w_up, w_down, mlp_in, mlp_bias, mlp_out, n, groups, total_count):
    toks, width = tokens.shape
    hidden = w_gate.shape[1]
    cap = -(-(3 * toks // n) // 16) * 16
    slots = n * cap
    colw = width // groups
    highs = groups // 2
    units = mlp_bias.shape[0]
    dma = pltpu.SemaphoreType.DMA
    vmem = pl.BlockSpec(memory_space=pltpu.VMEM)
    smem = pl.BlockSpec(memory_space=pltpu.SMEM)
    hbm = pl.BlockSpec(memory_space=pl.ANY)

    def v(*shape, dtype=BF16):
        return pltpu.VMEM(shape, dtype)

    def f(*shape):
        return pltpu.VMEM(shape, F32)

    lines = n + 8
    up_highs = max(highs - 1, 1)
    return pl.pallas_call(
        functools.partial(step_kernel, n, groups, cap, units, total_count),
        out_shape=(
            jax.ShapeDtypeStruct((toks, colw), BF16),
            jax.ShapeDtypeStruct((hidden, width), BF16),
            jax.ShapeDtypeStruct((n, width), BF16),
            jax.ShapeDtypeStruct((2, 8, LANES), F32),
            jax.ShapeDtypeStruct((width, hidden), F32),
            jax.ShapeDtypeStruct((width, hidden), F32),
        ),
        in_specs=[vmem] * 4 + [hbm] * 3 + [smem] * 3,
        out_specs=(vmem, hbm, vmem, vmem, hbm, hbm),
        scratch_shapes=[
            v(slots, toks), v(slots, toks), f(8, toks),
            v(slots, colw), v(slots, colw), v(slots, width), v(slots, width),
            v(width, hidden), v(width, hidden), v(hidden, width),
            v(slots, hidden), v(hidden, slots), v(width, slots),
            f(slots, hidden), f(slots, hidden), v(slots, 2 * hidden), f(slots, LANES),
            f(hidden, width), f(width, hidden), f(width, hidden),
            v(groups, slots, colw), v(highs, slots, colw), v(highs, slots, colw), v(highs, slots, colw),
            v(slots, colw), v(slots, colw),
            f(lines, LANES), f(groups, lines, LANES), f(lines, LANES), f(n, lines, LANES),
            f(16, LANES), f(groups, 16, LANES), f(16, LANES), f(n, 16, LANES),
            f(n, colw), f(n, n, colw), f(n, colw), f(groups, n, colw),
            v(hidden, width), f(5 * units + 1, 8, LANES), f(8, LANES), f(3, 8, LANES),
            dma((3,)), dma((3,)), dma((3,)),
            dma((4, n)), dma((4, up_highs, n)), dma((4, n)), dma((4, up_highs, n)),
            dma((2, highs)), dma((2, highs)), dma((2, n)),
            dma((2, groups)), dma((2, n)), dma((2, groups)), dma((2, n)), dma((2, n)), dma((2, groups)),
        ],
        compiler_params=pltpu.CompilerParams(
            collective_id=0, has_side_effects=True, vmem_limit_bytes=60 * 1024 * 1024
        ),
        name="fused_step",
    )(tokens, cot, routes, router, w_gate, w_up, w_down, mlp_in, mlp_bias, mlp_out)


def update_kernel(units, scale, inv_ref, mlp_in, mlp_bias, mlp_out, g_ref, w_ref, out_ref, table):
    rows, width = g_ref.shape
    strips = width // LANES

    @pl.when(pl.program_id(0) == 0)
    def _():
        fill_table(units, table, mlp_in, mlp_bias, mlp_out)

    def body(step):
        r = pl.ds(pl.multiple_of((step // strips) * CHUNK, CHUNK), CHUNK)
        c = lane(lax.rem(step, strips))
        f0 = g_ref[r, c] * tall(inv_ref[...], CHUNK)
        out_ref[r, c] = network(units, table, f0, w_ref[r, c].astype(F32) * scale)

    every(0, (rows // CHUNK) * strips, body)


def update(g, w, scale, inv, mlp_in, mlp_bias, mlp_out):
    units = mlp_bias.shape[0]
    rows, width = g.shape
    block = CHUNK
    smem = pl.BlockSpec(memory_space=pltpu.SMEM)
    return pl.pallas_call(
        functools.partial(update_kernel, units, scale),
        grid=(rows // block,),
        out_shape=jax.ShapeDtypeStruct((rows, width), BF16),
        in_specs=[
            pl.BlockSpec((8, LANES), lambda i: (0, 0)), smem, smem, smem,
            pl.BlockSpec((block, width), lambda i: (i, 0)),
            pl.BlockSpec((block, width), lambda i: (i, 0)),
        ],
        out_specs=pl.BlockSpec((block, width), lambda i: (i, 0)),
        scratch_shapes=[pltpu.VMEM((5 * units + 1, 8, LANES), F32)],
        cost_estimate=pl.CostEstimate(
            flops=rows * width * 9 * units, bytes_accessed=rows * width * 8, transcendentals=rows * width
        ),
        name="update",
    )(inv, mlp_in, mlp_bias, mlp_out, g, w)


def on_device(
    tokens, cotangent, routes, router_weight, gate_weight, up_weight, down_weight, mlp_in, mlp_bias, mlp_out
):
    n = lax.axis_size("expert")
    groups = lax.axis_size("mp")
    w_gate, w_up, w_down = gate_weight[0], up_weight[0], down_weight[0]
    width, hidden = w_gate.shape
    total_count = float(n * width * hidden * groups)
    mixed, down_update, router_update, inv, gate_grad, up_grad = fused_step(
        tokens, cotangent, routes.T, router_weight.T, w_gate, w_up, w_down,
        mlp_in, mlp_bias, mlp_out, n, groups, total_count,
    )
    net = (mlp_in, mlp_bias, mlp_out)
    gate_update = update(gate_grad, w_gate, float(width**0.5), inv[0], *net)
    up_update = update(up_grad, w_up, float(width**0.5), inv[1], *net)
    return (mixed, gate_update[None], up_update[None], down_update[None], router_update.T)


def solution(mesh):
    placed = (
        P("expert", None),
        P("expert", None),
        P("expert", None),
        P(),
        P("expert", None, "mp"),
        P("expert", None, "mp"),
        P("expert", "mp", None),
        P(),
        P(),
        P(),
    )
    return jax.shard_map(
        on_device,
        mesh=mesh,
        in_specs=placed,
        out_specs=(
            P("expert", "mp"),
            P("expert", None, "mp"),
            P("expert", None, "mp"),
            P("expert", "mp", None),
            P(),
        ),
        check_vma=False,
    )
```

time: 176 us -> 125 us (0.71)
  matrix products: 30.6 us -> 0 us
  other arithmetic: 11 us -> 0 us
  local copies, waits for them, and re-layouts: 11.4 us -> 3.78 us
  Pallas kernels: 117 us -> 120 us
  between operations: 3.63 us -> 0.65 us
  starting transfers between devices: 2.35 us -> 0 us
    dot_general x12 -> x0, matrix products: 30.6 us -> none  [the longest x1 5.79 us: on_device(): jnp.einsum('sd,sf->df', rows_x, d_up, preferred_element_type=jnp.float32)]
    convert_element_type x6 -> x0, other arithmetic: 4.63 us -> none  [the longest x1 2.18 us: on_device(): total_out.astype(jnp.bfloat16).reshape(experts, capacity, col_width)]
    pallas_call x6 -> x3, Pallas kernels: 117 us -> 120 us  [the longest x1 82.2 us: fused_step(): pl.pallas_call(functools.partial(step_kernel, n, groups, cap, units, tota...]
    slice x4 -> x0, local copies, waits for them, and re-layouts: 3.27 us -> none  [the longest x1 2.46 us: on_device(): rows_x = got[0].reshape(slots, width)]
    reduce_sum x8 -> x0, other arithmetic: 2.86 us -> none  [the longest x1 1.5 us: on_device(): jnp.sum(router_grad * router_grad) / (width * experts) + EPSILON]
    concatenate x1 -> x0, local copies, waits for them, and re-layouts: 2.51 us -> none  [on_device(): jnp.concatenate([inner, norms, jnp.zeros((lines * 128 - need,), jnp.float...]
    ppermute x3 -> x0, starting transfers between devices: 2.35 us -> none  [on_device(): lax.ppermute(piece, 'mp', [(m, (m + shift) % groups) for m in range(group...]
    another operation x3 -> x0, other arithmetic: 2.13 us -> none
  transfers between devices with their start and end apart: 3 -> 0, of which waited for: 0 -> 0; matrix products, arithmetic and copies ran while one was open for 2% -> 0% of each run, Pallas kernels for 24% -> 0%
where the time goes in v1:
time: 125 us
  Pallas kernels  120 us (96%)
  local copies, waits for them, and re-layouts  3.78 us (3%)
    pallas_call x1, Pallas kernels, fused_step(): pl.pallas_call(functools.partial(step_kernel, n, groups, cap, units, tota...  82.2 us
    pallas_call x2, Pallas kernels, update(): pl.pallas_call(functools.partial(update_kernel, units, scale), grid=(rows...  38.2 us
    unnamed x9, local copies, waits for them, and re-layouts  2.5 us

profile of v1, /device:TPU:0, one launch (start us, length us, event | category | flops | bytes accessed | tf_op | source)
XLA Modules:
  0.0 124.8 jit_solution(9856928740915202387)
XLA Ops:
  0.6 82.2 %fused_step.1 = (bf16[256,256]{1,0:T(8,128)(2,1)}, bf16[896,1024]{1,0:T(8,128)(2,1)}, bf16[8,1024]{1,0:T(8,128)(2,1)}, f32[2,8,128]{2,1,0:T(8,128)}, f32[1024,896]{1,0:T(8,128)}, /*index=5*/f32[1024,896]{1,0:T(8,128)}) custom-call(bf16[256,1024]{1,0:T(8,128)(2,1)} %tokens.1, bf16[256,1024]{1,0:T(8,128)(2,1)} %cot.1, s32[2,256]{1,0:T(2,128)} %bitcast.23, ...), custom_call_target="tpu_custom_call" | custom-call | tf_op jit(solution)/shard_map/fused_step/pallas_call | solution.py:516
  82.8 1.3 %slice_bitcast_fusion = (f32[8,128]{1,0:T(8,128)}, f32[8,128]{1,0:T(8,128)}) fusion(f32[2,8,128]{2,1,0:T(8,128)} %get-tuple-element.12), kind=kLoop, calls=%fused_computation | loop fusion | bytes 16384 | tf_op jit(solution)/shard_map/squeeze | solution.py:607
  84.1 19.0 %update.2 = bf16[1024,896]{1,0:T(8,128)(2,1)} custom-call(f32[8,128]{1,0:T(8,128)} %get-tuple-element.18.inv_ref, f32[3,16]{1,0:T(4,128)} %mlp_in.5, f32[16]{0:T(128)} %mlp_bias.5, f32[16]{0:T(128)} %mlp_out.5, f32[1024,896]{1,0:T(8,128)} %get-tuple-element.13.g_ref, bf16[1024,896]{1,0:T(8,128)(2,1)} %bitcast.14), custom_call_target="tpu_custom_call" | custom-call | flops 132120576 | bytes 7340032 | tf_op jit(solution)/shard_map/update/pallas_call | solution.py:575
  103.1 0.0 copy-start.1
  103.1 0.0 copy-start
  103.1 19.2 %update.3 = bf16[1024,896]{1,0:T(8,128)(2,1)} custom-call(f32[8,128]{1,0:T(8,128)} %get-tuple-element.17.inv_ref, f32[3,16]{1,0:T(4,128)} %mlp_in.5, f32[16]{0:T(128)} %mlp_bias.5, f32[16]{0:T(128)} %mlp_out.5, f32[1024,896]{1,0:T(8,128)} %get-tuple-element.14.g_ref, bf16[1024,896]{1,0:T(8,128)(2,1)} %bitcast.16), custom_call_target="tpu_custom_call" | custom-call | flops 132120576 | bytes 7340032 | tf_op jit(solution)/shard_map/update/pallas_call | solution.py:575
  122.3 0.0 copy-done.1
  122.3 0.7 copy.18
  123.0 0.0 copy-done
  123.0 0.0 copy-start.2
  123.0 1.2 copy.19
  124.2 0.0 copy-done.2
  124.2 0.6 copy.20
Async XLA Ops:
  103.1 19.2 %copy-start.1 = (bf16[256,256]{1,0:T(8,128)(2,1)S(1)}, bf16[256,256]{1,0:T(8,128)(2,1)}, u32[]{:S(2)}) copy-start(bf16[256,256]{1,0:T(8,128)(2,1)} %get-tuple-element.24) | copy-start | bytes 393220
  103.1 19.8 %copy-start = (bf16[896,1024]{1,0:T(8,128)(2,1)S(1)}, bf16[896,1024]{1,0:T(8,128)(2,1)}, u32[]{:S(2)}) copy-start(bf16[896,1024]{1,0:T(8,128)(2,1)} %get-tuple-element.15) | copy-start | bytes 5505028
  123.0 1.2 copy-start.2

commit v2 on v1

--- a/solution.py
+++ b/solution.py
@@ -102,12 +102,13 @@
 
 def step_kernel(
     n, groups, cap, units, total_count,
-    tokens, cot, routes, router, gate_hbm, up_hbm, down_hbm, mlp_in, mlp_bias, mlp_out,
-    mixed_ref, down_out, router_out, inv_out, gate_grad, up_grad,
+    tokens_hbm, cot_hbm, routes_hbm, router_hbm, gate_hbm, up_hbm, down_hbm, mlp_in, mlp_bias, mlp_out,
+    mixed_ref, down_out, router_out, inv_gate, inv_up, gate_grad, up_grad,
+    tokens, cot, routes, router,
     m0, m1, gates, sx, sdy, rx, rdy, vg, vu, vd, hid, hid_t, rx_t, silu, slope, dcat, inner,
     gd, gg, gu, part, prec, psum, hrec, back, ret, parcel, pmp, psend, pex, norms, nmp, nsend, nex,
     rpart, rex, rsum, rmp, dout, table, inv_down, squared,
-    wsem, own, osem, xsem, xhigh, ysem, yhigh, lowsem, highsem, retsem, psem, pesem, nsem, nesem, rsem, rmsem,
+    isem, wsem, own, osem, xsem, xhigh, ysem, yhigh, lowsem, highsem, retsem, psem, pesem, nsem, nesem, rsem, rmsem,
 ):
     me = lax.axis_index("expert")
     col = lax.axis_index("mp")
@@ -117,7 +118,6 @@
     highs = groups // 2
     toks, width = tokens.shape
     colw = width // groups
-    slots = n * cap
     hidden = vg.shape[1]
     tiles = hidden // LANES
     cols = lane(col, colw)
@@ -149,6 +149,10 @@
     every(1, n, greet)
     every(1, groups, greet_mp)
 
+    pairs = ((tokens_hbm, tokens), (cot_hbm, cot), (routes_hbm, routes), (router_hbm, router))
+    inputs = [pltpu.make_async_copy(src, dst, isem.at[k]) for k, (src, dst) in enumerate(pairs)]
+    for k in (2, 0, 3, 1):
+        inputs[k].start()
     loads = [
         pltpu.make_async_copy(gate_hbm, vg, wsem.at[0]),
         pltpu.make_async_copy(up_hbm, vu, wsem.at[1]),
@@ -157,6 +161,7 @@
     for load in loads:
         load.start()
 
+    inputs[2].wait()
     r0, r1 = routes[0:1, :], routes[1:2, :]
     rank = max(n, 16)
     ids = lax.broadcasted_iota(jnp.int32, (rank, toks), 0)
@@ -171,6 +176,7 @@
         m0[e * cap : (e + 1) * cap, :] = jnp.where(hit & (r0 == e), 1.0, 0.0).astype(BF16)
         m1[e * cap : (e + 1) * cap, :] = jnp.where(hit & (r1 == e), 1.0, 0.0).astype(BF16)
     both = m0[...] + m1[...]
+    inputs[0].wait()
     sx[...] = dot(both, tokens[:, cols]).astype(BF16)
 
     def exchange(send, out, sem, high):
@@ -203,17 +209,8 @@
                 forward(h, i).start()
 
         def step(i):
-            @pl.when((i > 0) & (i < n))
-            def _():
-                spread(i).wait_recv()
-
-            @pl.when(i < n)
-            def _():
-                share(i)
-
-            @pl.when(i > 0)
-            def _():
-                relay(i - 1)
+            spread(i).wait_recv()
+            share(i)
 
         def arrived(i):
             low(i).wait_recv()
@@ -226,16 +223,19 @@
                 far(h, i).wait_send()
                 forward(h, i).wait_send()
 
-        return spread, step, arrived, sent
-
-    spread_x, step_x, arrived_x, sent_x = exchange(sx, rx, xsem, xhigh)
-    spread_y, step_y, arrived_y, sent_y = exchange(sdy, rdy, ysem, yhigh)
+        return spread, share, step, relay, arrived, sent
+
+    spread_x, share_x, step_x, relay_x, arrived_x, sent_x = exchange(sx, rx, xsem, xhigh)
+    spread_y, share_y, step_y, relay_y, arrived_y, sent_y = exchange(sdy, rdy, ysem, yhigh)
 
     pl.semaphore_wait(barrier, n - 1 + groups - 1)
     every(1, n, lambda i: spread_x(i).start())
     own_x = pltpu.make_async_copy(sx.at[rows(me)], rx.at[rows(me), cols], own.at[0])
     own_x.start()
 
+    own_x.wait()
+    share_x(0)
+    inputs[3].wait()
     logits = dot_nt(router[...], tokens[...])
     kinds = lax.broadcasted_iota(jnp.int32, (n, toks), 0)
     sigma0 = jax.nn.sigmoid(jnp.sum(jnp.where(kinds == r0, logits, 0.0), axis=0, keepdims=True))
@@ -247,21 +247,25 @@
     weight = jnp.sum(
         m0[...].astype(F32) * gates[0:1, :] + m1[...].astype(F32) * gates[1:2, :], axis=1, keepdims=True
     )
+    inputs[1].wait()
     sdy[...] = (weight * dot(both, cot[:, cols])).astype(BF16)
-    own_x.wait()
     every(1, n, lambda i: spread_y(i).start())
     own_y = pltpu.make_async_copy(sdy.at[rows(me)], rdy.at[rows(me), cols], own.at[1])
     own_y.start()
     fill_table(units, table, mlp_in, mlp_bias, mlp_out)
 
-    every(0, n + 1, step_x)
-    every(0, n, arrived_x)
+    every(1, n, step_x)
+    every(0, n, relay_x)
     own_y.wait()
+    share_y(0)
+    early = n // 2
+    every(1, early, step_y)
     for load in loads:
         load.wait()
+    every(0, n, arrived_x)
 
     def forward_tile(j):
-        every(j * (n + 1) // tiles, (j + 1) * (n + 1) // tiles, step_y)
+        every(early + j * (n - early) // tiles, early + (j + 1) * (n - early) // tiles, step_y)
         c = lane(j)
         act = dot(rx[...], jnp.concatenate([vg[:, c], vu[:, c]], axis=1))
         act_gate, act_up = act[:, :LANES], act[:, LANES:]
@@ -279,6 +283,7 @@
         rx_t[lane(j), :] = rx[:, lane(j)].astype(F32).T.astype(BF16)
 
     every(0, width // LANES, turn)
+    every(0, n, relay_y)
 
     def partial(m):
         part[m] = dot(hid[...], vd[:, lane(m, colw)]).astype(BF16)
@@ -368,9 +373,10 @@
     puts = [
         pltpu.make_async_copy(gg, gate_grad, osem.at[0]),
         pltpu.make_async_copy(gu, up_grad, osem.at[1]),
+        pltpu.make_async_copy(dout, down_out, osem.at[2]),
     ]
-    for put in puts:
-        put.start()
+    puts[0].start()
+    puts[1].start()
     norms[0:8, :] = squared[1]
     norms[8:16, :] = squared[2]
     every(1, groups, lambda i: across(norms, nmp, nsem, i).start())
@@ -417,7 +423,7 @@
     every(1, n, lambda i: around(rpart, rex, rsem, i).start())
     rex[me] = rpart[...]
 
-    update_band(marks[1], marks[3])
+    update_band(marks[1], marks[2])
 
     every(1, highs, lambda h: lend(h).wait_recv())
     summed = part[col].astype(F32) + prec[pair].astype(F32)
@@ -433,7 +439,7 @@
     own_r = pltpu.make_async_copy(back.at[rows(me)], ret.at[rows(me)], own.at[2])
     own_r.start()
 
-    update_band(marks[3], marks[4])
+    update_band(marks[2], marks[4])
     every(1, n, lambda i: around(rpart, rex, rsem, i).wait_recv())
     rsum[...] = total_of(rex, n)
     every(1, groups, lambda i: across(rsum, rmp, rmsem, i).start())
@@ -442,8 +448,8 @@
     update_band(marks[4], marks[5])
     every(1, n, lambda i: around(nsend, nex, nesem, i).wait_recv())
     both_norms = total_of(nex, n)
-    inv_out[0] = inverse_rms(both_norms[0:8, :], total_count)
-    inv_out[1] = inverse_rms(both_norms[8:16, :], total_count)
+    inv_gate[...] = inverse_rms(both_norms[0:8, :], total_count)
+    inv_up[...] = inverse_rms(both_norms[8:16, :], total_count)
 
     update_band(marks[5], marks[6])
     every(1, groups, lambda i: across(rsum, rmp, rmsem, i).wait_recv())
@@ -459,8 +465,7 @@
             router_out[:, c] = network(units, table, f0, router[:, c].astype(F32) * float(width**0.5))
 
     update_band(marks[6], marks[7])
-    puts.append(pltpu.make_async_copy(dout, down_out, osem.at[2]))
-    puts[-1].start()
+    puts[2].start()
 
     own_r.wait()
     every(1, n, lambda i: bring(i).wait_recv())
@@ -519,13 +524,15 @@
             jax.ShapeDtypeStruct((toks, colw), BF16),
             jax.ShapeDtypeStruct((hidden, width), BF16),
             jax.ShapeDtypeStruct((n, width), BF16),
-            jax.ShapeDtypeStruct((2, 8, LANES), F32),
+            jax.ShapeDtypeStruct((8, LANES), F32),
+            jax.ShapeDtypeStruct((8, LANES), F32),
             jax.ShapeDtypeStruct((width, hidden), F32),
             jax.ShapeDtypeStruct((width, hidden), F32),
         ),
-        in_specs=[vmem] * 4 + [hbm] * 3 + [smem] * 3,
-        out_specs=(vmem, hbm, vmem, vmem, hbm, hbm),
+        in_specs=[hbm] * 7 + [smem] * 3,
+        out_specs=(vmem, hbm, vmem, vmem, vmem, hbm, hbm),
         scratch_shapes=[
+            v(toks, width), v(toks, width), pltpu.VMEM((2, toks), jnp.int32), v(n, width),
             v(slots, toks), v(slots, toks), f(8, toks),
             v(slots, colw), v(slots, colw), v(slots, width), v(slots, width),
             v(width, hidden), v(width, hidden), v(hidden, width),
@@ -538,7 +545,7 @@
             f(16, LANES), f(groups, 16, LANES), f(16, LANES), f(n, 16, LANES),
             f(n, colw), f(n, n, colw), f(n, colw), f(groups, n, colw),
             v(hidden, width), f(5 * units + 1, 8, LANES), f(8, LANES), f(3, 8, LANES),
-            dma((3,)), dma((3,)), dma((3,)),
+            dma((4,)), dma((3,)), dma((3,)), dma((3,)),
             dma((4, n)), dma((4, up_highs, n)), dma((4, n)), dma((4, up_highs, n)),
             dma((2, highs)), dma((2, highs)), dma((2, n)),
             dma((2, groups)), dma((2, n)), dma((2, groups)), dma((2, n)), dma((2, n)), dma((2, groups)),
@@ -550,44 +557,140 @@
     )(tokens, cot, routes, router, w_gate, w_up, w_down, mlp_in, mlp_bias, mlp_out)
 
 
-def update_kernel(units, scale, inv_ref, mlp_in, mlp_bias, mlp_out, g_ref, w_ref, out_ref, table):
-    rows, width = g_ref.shape
-    strips = width // LANES
-
-    @pl.when(pl.program_id(0) == 0)
-    def _():
-        fill_table(units, table, mlp_in, mlp_bias, mlp_out)
-
-    def body(step):
-        r = pl.ds(pl.multiple_of((step // strips) * CHUNK, CHUNK), CHUNK)
-        c = lane(lax.rem(step, strips))
-        f0 = g_ref[r, c] * tall(inv_ref[...], CHUNK)
-        out_ref[r, c] = network(units, table, f0, w_ref[r, c].astype(F32) * scale)
-
-    every(0, (rows // CHUNK) * strips, body)
-
-
-def update(g, w, scale, inv, mlp_in, mlp_bias, mlp_out):
+def ordered_table(units, table, mlp_in, mlp_bias, mlp_out, inv, scale):
+    outs = [mlp_out[j] for j in range(units)]
+    above = [(out > 0.0).astype(jnp.int32) for out in outs]
+    positive = sum(above)
+    seen = jnp.int32(0)
+    total = jnp.zeros((8, LANES), F32)
+    for j in range(units):
+        slot = jnp.where(above[j] > 0, seen, positive + j - seen)
+        seen = seen + above[j]
+        size = jnp.full((8, LANES), jnp.abs(outs[j]), F32)
+        bias = jnp.full((8, LANES), mlp_bias[j], F32)
+        table[slot] = size * jnp.full((8, LANES), mlp_in[0, j], F32) * inv
+        table[units + slot] = size * jnp.full((8, LANES), mlp_in[1, j] * scale, F32)
+        table[2 * units + slot] = size * jnp.full((8, LANES), mlp_in[2, j], F32)
+        table[3 * units + slot] = -(size * bias)
+        table[4 * units + slot] = jnp.full((8, LANES), jnp.where(outs[j] > 0.0, 1.0, -1.0), F32)
+        total = total + jnp.full((8, LANES), outs[j], F32) * bias
+    table[5 * units] = total
+    table[5 * units + 1] = inv
+    return positive
+
+
+def ordered_network(units, table, sure, g, w):
+    rows = g.shape[0]
+
+    def coef(i):
+        return tall(table[i], rows)
+
+    f2 = jnp.tanh(g * coef(5 * units + 1))
+    acc = coef(5 * units)
+    for j in range(units):
+        y = coef(j) * g + coef(units + j) * w + coef(2 * units + j) * f2
+        part = jnp.maximum(y, coef(3 * units + j))
+        if j < sure:
+            acc = acc + part
+        elif j == sure:
+            acc = acc + coef(4 * units + j) * part
+        else:
+            acc = acc - part
+    return acc.astype(BF16)
+
+
+def update_kernel(
+    units, scale, gate_grad, up_grad, gate_hbm, up_hbm, inv_gate, inv_up, mlp_in, mlp_bias, mlp_out,
+    gate_out, up_out, gate_g, up_g, gate_w, up_w, gate_new, up_new, table, gsem, wsem, osem,
+):
+    width, hidden = gate_grad.shape
+    strips = hidden // LANES
+    bands = width // CHUNK
+
+    def rows(b):
+        return pl.ds(pl.multiple_of(b * CHUNK, CHUNK), CHUNK)
+
+    def load(k, b):
+        r = rows(b)
+        g, g_ref, w, w_ref = ((gate_grad, gate_g, gate_hbm, gate_w), (up_grad, up_g, up_hbm, up_w))[k]
+        return (
+            pltpu.make_async_copy(g.at[r], g_ref.at[r], gsem.at[k, b]),
+            pltpu.make_async_copy(w.at[r], w_ref.at[r], wsem.at[k, b]),
+        )
+
+    def begin(k, b):
+        for copy in load(k, b):
+            copy.start()
+
+    every(0, bands, lambda b: begin(0, b))
+    every(0, bands, lambda b: begin(1, b))
+
+    def tensor(k, g_ref, w_ref, inv, new, out):
+        positive = ordered_table(units, table, mlp_in, mlp_bias, mlp_out, inv[...], scale)
+
+        def put(b):
+            return pltpu.make_async_copy(new.at[rows(b)], out.at[rows(b)], osem.at[k, b])
+
+        for sure in range(0, units + 1, 2):
+
+            @pl.when(positive // 2 == sure // 2)
+            def _():
+                def band(b):
+                    r = rows(b)
+                    for copy in load(k, b):
+                        copy.wait()
+
+                    def strip(c):
+                        new[r, lane(c)] = ordered_network(
+                            units, table, sure, g_ref[r, lane(c)], w_ref[r, lane(c)].astype(F32)
+                        )
+
+                    every(0, strips, strip)
+                    put(b).start()
+
+                every(0, bands, band)
+
+        return put
+
+    puts = [
+        tensor(0, gate_g, gate_w, inv_gate, gate_new, gate_out),
+        tensor(1, up_g, up_w, inv_up, up_new, up_out),
+    ]
+    for put in puts:
+        every(0, bands, lambda b: put(b).wait())
+
+
+def update(gate_grad, up_grad, w_gate, w_up, inv_gate, inv_up, mlp_in, mlp_bias, mlp_out):
     units = mlp_bias.shape[0]
-    rows, width = g.shape
-    block = CHUNK
+    width, hidden = gate_grad.shape
     smem = pl.BlockSpec(memory_space=pltpu.SMEM)
+    vmem = pl.BlockSpec(memory_space=pltpu.VMEM)
+    hbm = pl.BlockSpec(memory_space=pl.ANY)
+    shape = jax.ShapeDtypeStruct((width, hidden), BF16)
     return pl.pallas_call(
-        functools.partial(update_kernel, units, scale),
-        grid=(rows // block,),
-        out_shape=jax.ShapeDtypeStruct((rows, width), BF16),
-        in_specs=[
-            pl.BlockSpec((8, LANES), lambda i: (0, 0)), smem, smem, smem,
-            pl.BlockSpec((block, width), lambda i: (i, 0)),
-            pl.BlockSpec((block, width), lambda i: (i, 0)),
+        functools.partial(update_kernel, units, float(width**0.5)),
+        out_shape=(shape, shape),
+        in_specs=[hbm] * 4 + [vmem] * 2 + [smem] * 3,
+        out_specs=(hbm, hbm),
+        scratch_shapes=[
+            pltpu.VMEM((width, hidden), F32),
+            pltpu.VMEM((width, hidden), F32),
+            pltpu.VMEM((width, hidden), BF16),
+            pltpu.VMEM((width, hidden), BF16),
+            pltpu.VMEM((width, hidden), BF16),
+            pltpu.VMEM((width, hidden), BF16),
+            pltpu.VMEM((5 * units + 2, 8, LANES), F32),
+            pltpu.SemaphoreType.DMA((2, width // CHUNK)),
+            pltpu.SemaphoreType.DMA((2, width // CHUNK)),
+            pltpu.SemaphoreType.DMA((2, width // CHUNK)),
         ],
-        out_specs=pl.BlockSpec((block, width), lambda i: (i, 0)),
-        scratch_shapes=[pltpu.VMEM((5 * units + 1, 8, LANES), F32)],
+        compiler_params=pltpu.CompilerParams(vmem_limit_bytes=60 * 1024 * 1024),
         cost_estimate=pl.CostEstimate(
-            flops=rows * width * 9 * units, bytes_accessed=rows * width * 8, transcendentals=rows * width
+            flops=2 * width * hidden * 9 * units, bytes_accessed=4 * width * hidden,
+            transcendentals=2 * width * hidden,
         ),
         name="update",
-    )(inv, mlp_in, mlp_bias, mlp_out, g, w)
+    )(gate_grad, up_grad, w_gate, w_up, inv_gate, inv_up, mlp_in, mlp_bias, mlp_out)
 
 
 def on_device(
@@ -598,13 +701,13 @@
     w_gate, w_up, w_down = gate_weight[0], up_weight[0], down_weight[0]
     width, hidden = w_gate.shape
     total_count = float(n * width * hidden * groups)
-    mixed, down_update, router_update, inv, gate_grad, up_grad = fused_step(
+    mixed, down_update, router_update, inv_gate, inv_up, gate_grad, up_grad = fused_step(
         tokens, cotangent, routes.T, router_weight.T, w_gate, w_up, w_down,
         mlp_in, mlp_bias, mlp_out, n, groups, total_count,
     )
-    net = (mlp_in, mlp_bias, mlp_out)
-    gate_update = update(gate_grad, w_gate, float(width**0.5), inv[0], *net)
-    up_update = update(up_grad, w_up, float(width**0.5), inv[1], *net)
+    gate_update, up_update = update(
+        gate_grad, up_grad, w_gate, w_up, inv_gate, inv_up, mlp_in, mlp_bias, mlp_out
+    )
     return (mixed, gate_update[None], up_update[None], down_update[None], router_update.T)
 
 

time: 125 us -> 109 us (0.87)
  Pallas kernels: 120 us -> 106 us
  local copies, waits for them, and re-layouts: 3.78 us -> 2.5 us
    pallas_call x1, Pallas kernels: 82.2 us -> 72.9 us  [fused_step(): pl.pallas_call(functools.partial(step_kernel, n, groups, cap, units, tota...]
    pallas_call x2 -> x1, Pallas kernels: 38.2 us -> 32.9 us  [update(): pl.pallas_call(functools.partial(update_kernel, units, float(width ** 0.5...]
    squeeze x1 -> x0, local copies, waits for them, and re-layouts: 1.28 us -> none  [on_device(): up_update = update(up_grad, w_up, float(width ** 0.5), inv[1], *net)]
where the time goes in v2:
time: 109 us
  Pallas kernels  106 us (97%)
  local copies, waits for them, and re-layouts  2.5 us (2%)
    pallas_call x1, Pallas kernels, fused_step(): pl.pallas_call(functools.partial(step_kernel, n, groups, cap, units, tota...  72.9 us
    pallas_call x1, Pallas kernels, update(): pl.pallas_call(functools.partial(update_kernel, units, float(width ** 0.5...  32.9 us
    unnamed x9, local copies, waits for them, and re-layouts  2.5 us

profile of v2, /device:TPU:0, one launch (start us, length us, event | category | flops | bytes accessed | tf_op | source)
XLA Modules:
  0.0 109.0 jit_solution(12452140822895175715)
XLA Ops:
  0.6 72.9 %fused_step.1 = (bf16[256,256]{1,0:T(8,128)(2,1)}, bf16[896,1024]{1,0:T(8,128)(2,1)}, bf16[8,1024]{1,0:T(8,128)(2,1)}, f32[8,128]{1,0:T(8,128)}, f32[8,128]{1,0:...) custom-call(bf16[256,1024]{1,0:T(8,128)(2,1)} %tokens_hbm.1, bf16[256,1024]{1,0:T(8,128)(2,1)} %cot_hbm.1, ...), custom_call_target="tpu_custom_call" | custom-call | tf_op jit(solution)/shard_map/fused_step/pallas_call | solution.py:521
  73.6 0.0 copy-start.1
  73.6 0.0 copy-start
  73.6 32.9 %update.1 = (bf16[1024,896]{1,0:T(8,128)(2,1)}, bf16[1024,896]{1,0:T(8,128)(2,1)}) custom-call(f32[1024,896]{1,0:T(8,128)} %get-tuple-element.15.gate_grad, f32[1024,896]{1,0:T(8,128)} %get-tuple-element.16.up_grad, bf16[1024,896]{1,0:T(8,128)(2,1)} %bitcast.10, bf16[1024,896]{1,0:T(8,128)(2,1)} %bitcast.12, f32[8,128]{1,0:T(8,128)} %get-tuple-element.17.inv_gate, ...), custom_call_target="tpu_custom_call" | custom-call | flops 264241152 | bytes 3670016 | tf_op jit(solution)/shard_map/update/pallas_call | solution.py:670
  106.5 0.0 copy-done.1
  106.5 0.7 copy.18
  107.1 0.0 copy-done
  107.2 0.0 copy-start.2
  107.2 1.2 %copy.19 = bf16[1,896,1024]{2,1,0:T(8,128)(2,1)} copy(bf16[1,896,1024]{2,1,0:T(8,128)(2,1)S(1)} %bitcast.13) | data formatting | bytes 3670016
  108.4 0.0 copy-done.2
  108.4 0.6 copy.20
Async XLA Ops:
  73.6 32.9 %copy-start.1 = (bf16[256,256]{1,0:T(8,128)(2,1)S(1)}, bf16[256,256]{1,0:T(8,128)(2,1)}, u32[]{:S(2)}) copy-start(bf16[256,256]{1,0:T(8,128)(2,1)} %get-tuple-element.28) | copy-start | bytes 393220
  73.6 33.6 %copy-start = (bf16[896,1024]{1,0:T(8,128)(2,1)S(1)}, bf16[896,1024]{1,0:T(8,128)(2,1)}, u32[]{:S(2)}) copy-start(bf16[896,1024]{1,0:T(8,128)(2,1)} %get-tuple-element.21) | copy-start | bytes 5505028
  107.2 1.2 %copy-start.2 = (bf16[8,1024]{1,0:T(8,128)(2,1)S(1)}, bf16[8,1024]{1,0:T(8,128)(2,1)}, u32[]{:S(2)}) copy-start(bf16[8,1024]{1,0:T(8,128)(2,1)} %get-tuple-element.22) | copy-start | bytes 49156

commit v3 on v2

--- a/solution.py
+++ b/solution.py
@@ -44,30 +44,49 @@
 
 
 def fill_table(units, table, mlp_in, mlp_bias, mlp_out):
+    def splat(value):
+        return jnp.full((8, LANES), value, F32)
+
+    outs = [splat(mlp_out[j]) for j in range(units)]
+    above = [jnp.where(out > 0.0, 1.0, 0.0) for out in outs]
+    positive = above[0]
+    for j in range(1, units):
+        positive = positive + above[j]
+    flipped = positive < units / 2
+    turn = jnp.where(flipped, -1.0, 1.0)
+    first = [jnp.where(flipped, 1.0 - a, a) for a in above]
+    leading = jnp.where(flipped, units - positive, positive)
+    slots, seen = [], jnp.zeros((8, LANES), F32)
     total = jnp.zeros((8, LANES), F32)
     for j in range(units):
-        bias = jnp.full((8, LANES), mlp_bias[j], F32)
-        out = jnp.full((8, LANES), mlp_out[j], F32)
-        for k in range(3):
-            table[k * units + j] = jnp.full((8, LANES), mlp_in[k, j], F32)
-        table[3 * units + j] = -bias
-        table[4 * units + j] = out
-        total = total + out * bias
-    table[5 * units] = total
-
-
-def network(units, table, f0, f1):
-    rows = f0.shape[0]
-
-    def coef(i):
-        return jnp.concatenate([table[i]] * (rows // 8), axis=0)
-
-    f2 = jnp.tanh(f0)
-    acc = coef(5 * units)
+        slots.append(jnp.where(first[j] > 0.0, seen, leading + j - seen))
+        seen = seen + first[j]
+        total = total + outs[j] * splat(mlp_bias[j])
+
+    def place(r):
+        zero = jnp.zeros((8, LANES), F32)
+        sums = [zero] * 5
+        for j in range(units):
+            here = slots[j] == r.astype(F32)
+            size = jnp.abs(outs[j])
+            values = [size * splat(mlp_in[k, j]) for k in range(3)]
+            values += [-(size * splat(mlp_bias[j])), 2.0 * first[j] - 1.0]
+            sums = [a + jnp.where(here, v, zero) for a, v in zip(sums, values)]
+        for k in range(5):
+            table[k * units + r] = sums[k]
+
+    every(0, units, place)
+    table[5 * units] = turn * total
+    table[5 * units + 1] = jnp.ones((8, LANES), F32)
+    table[5 * units + 2] = turn
+
+
+def fold_table(units, table, folded, inv, scale):
+    folded[...] = table[...]
     for j in range(units):
-        y = coef(j) * f0 + coef(units + j) * f1 + coef(2 * units + j) * f2
-        acc = acc + coef(4 * units + j) * jnp.maximum(y, coef(3 * units + j))
-    return acc.astype(BF16)
+        folded[j] = table[j] * inv
+        folded[units + j] = table[units + j] * scale
+    folded[5 * units + 1] = inv
 
 
 def inverse_rms(tile, count):
@@ -77,6 +96,26 @@
 
 def tall(tile, rows):
     return jnp.concatenate([tile] * (rows // 8), axis=0)
+
+
+def network(units, table, sure, signed, g, w):
+    rows = g.shape[0]
+
+    def coef(i):
+        return tall(table[i], rows)
+
+    f2 = jnp.tanh(g * coef(5 * units + 1))
+    acc = coef(5 * units)
+    for j in range(units):
+        y = coef(j) * g + coef(units + j) * w + coef(2 * units + j) * f2
+        part = jnp.maximum(y, coef(3 * units + j))
+        if j < sure:
+            acc = acc + part
+        elif j < sure + signed:
+            acc = acc + coef(4 * units + j) * part
+        else:
+            acc = acc - part
+    return acc
 
 
 def to_row(column):
@@ -106,8 +145,8 @@
     mixed_ref, down_out, router_out, inv_gate, inv_up, gate_grad, up_grad,
     tokens, cot, routes, router,
     m0, m1, gates, sx, sdy, rx, rdy, vg, vu, vd, hid, hid_t, rx_t, silu, slope, dcat, inner,
-    gd, gg, gu, part, prec, psum, hrec, back, ret, parcel, pmp, psend, pex, norms, nmp, nsend, nex,
-    rpart, rex, rsum, rmp, dout, table, inv_down, squared,
+    gd, gg, gu, part, prec, psum, hrec, back, ret, parcel, pmp, psend, pex, norm_down, dmp, dsend, dex,
+    rpart, rex, rsum, rmp, dout, table, folded, squared,
     isem, wsem, own, osem, xsem, xhigh, ysem, yhigh, lowsem, highsem, retsem, psem, pesem, nsem, nesem, rsem, rmsem,
 ):
     me = lax.axis_index("expert")
@@ -254,18 +293,22 @@
     own_y.start()
     fill_table(units, table, mlp_in, mlp_bias, mlp_out)
 
-    every(1, n, step_x)
-    every(0, n, relay_x)
     own_y.wait()
     share_y(0)
-    early = n // 2
-    every(1, early, step_y)
+    early, near = n // 2, n // 4
+    pace = -(-(n - early) * 2 // tiles)
+    every(1, early, step_x)
+    every(1, near, step_y)
+    every(early, n, step_x)
+    every(0, early, relay_x)
+    every(near, early, step_y)
+    every(early, n, relay_x)
     for load in loads:
         load.wait()
     every(0, n, arrived_x)
 
     def forward_tile(j):
-        every(early + j * (n - early) // tiles, early + (j + 1) * (n - early) // tiles, step_y)
+        every(jnp.minimum(early + j * pace, n), jnp.minimum(early + (j + 1) * pace, n), step_y)
         c = lane(j)
         act = dot(rx[...], jnp.concatenate([vg[:, c], vu[:, c]], axis=1))
         act_gate, act_up = act[:, :LANES], act[:, LANES:]
@@ -282,19 +325,63 @@
     def turn(j):
         rx_t[lane(j), :] = rx[:, lane(j)].astype(F32).T.astype(BF16)
 
+    every(0, early, relay_y)
     every(0, width // LANES, turn)
-    every(0, n, relay_y)
 
     def partial(m):
         part[m] = dot(hid[...], vd[:, lane(m, colw)]).astype(BF16)
 
-    every(0, groups, partial)
+    every(0, highs, partial)
+    every(early, n, relay_y)
+    every(highs, groups, partial)
 
     def give(q):
         return remote(part.at[2 * q + 1 - parity], prec.at[q], lowsem.at[0, q], lowsem.at[1, q], me, partner)
 
     every(0, highs, lambda q: give(q).start())
     every(0, n, arrived_y)
+
+    def across(src, dst, sem, i):
+        return remote(src, dst.at[col], sem.at[0, i], sem.at[1, i], me, lax.rem(col + i, groups))
+
+    def around(src, dst, sem, i):
+        return remote(src, dst.at[me], sem.at[0, i], sem.at[1, i], peer_to(i), col)
+
+    def total_of(ref, count):
+        acc = ref[0]
+        for i in range(1, count):
+            acc = acc + ref[i]
+        return acc
+
+    squared[...] = jnp.zeros_like(squared)
+
+    def down_tile(m):
+        c = lane(m, 2 * LANES)
+        g = dot(hid_t[...], rdy[:, c])
+        gd[:, c] = g
+        squared[0] += squares(g[:, :LANES]) + squares(g[:, LANES:])
+
+    every(0, width // (2 * LANES), down_tile)
+    norm_down[...] = squared[0]
+    every(1, groups, lambda i: across(norm_down, dmp, psem, i).start())
+    dmp[col] = norm_down[...]
+
+    every(0, highs, lambda q: give(q).wait_recv())
+
+    def lend(h, k):
+        q = lax.rem(pair + h, highs)
+        part_rows = pl.ds(k * (n * cap // 2), n * cap // 2)
+        return remote(
+            psum.at[q, part_rows], hrec.at[pair, part_rows],
+            highsem.at[0, k, h], highsem.at[1, k, h], me, 2 * q + parity,
+        )
+
+    def lend_first(h):
+        q = lax.rem(pair + h, highs)
+        psum[q] = (part[2 * q + parity].astype(F32) + prec[q].astype(F32)).astype(BF16)
+        lend(h, 0).start()
+
+    every(1, highs, lend_first)
 
     inner[...] = jnp.zeros_like(inner)
 
@@ -312,48 +399,13 @@
     every(0, hidden // (2 * LANES), lambda j: back_tile(j * 2 * LANES, 2 * LANES))
     if hidden % (2 * LANES):
         back_tile(hidden - LANES, LANES)
-
-    squared[...] = jnp.zeros_like(squared)
-
-    def down_tile(m):
-        c = lane(m, 2 * LANES)
-        g = dot(hid_t[...], rdy[:, c])
-        gd[:, c] = g
-        squared[0] += squares(g[:, :LANES]) + squares(g[:, LANES:])
-
-    every(0, width // (2 * LANES), down_tile)
-
     for e in range(n):
         parcel[e : e + 1, :] = to_row(jnp.sum(inner[e * cap : (e + 1) * cap, :], axis=1, keepdims=True))
-    parcel[n : n + 8, :] = squared[0]
-
-    def across(src, dst, sem, i):
-        return remote(src, dst.at[col], sem.at[0, i], sem.at[1, i], me, lax.rem(col + i, groups))
-
-    def around(src, dst, sem, i):
-        return remote(src, dst.at[me], sem.at[0, i], sem.at[1, i], peer_to(i), col)
-
-    every(1, groups, lambda i: across(parcel, pmp, psem, i).start())
-    pmp[col] = parcel[...]
-
-    def total_of(ref, count):
-        acc = ref[0]
-        for i in range(1, count):
-            acc = acc + ref[i]
-        return acc
-
-    every(0, highs, lambda q: give(q).wait_recv())
-
-    def lend(h):
-        q = lax.rem(pair + h, highs)
-        return remote(psum.at[q], hrec.at[pair], highsem.at[0, h], highsem.at[1, h], me, 2 * q + parity)
-
-    def lend_all(h):
-        q = lax.rem(pair + h, highs)
-        psum[q] = (part[2 * q + parity].astype(F32) + prec[q].astype(F32)).astype(BF16)
-        lend(h).start()
-
-    every(1, highs, lend_all)
+
+    every(1, groups, lambda i: across(norm_down, dmp, psem, i).wait_recv())
+    dsend[...] = total_of(dmp, groups)
+    every(1, n, lambda i: around(dsend, dex, pesem, i).start())
+    dex[me] = dsend[...]
 
     def grad_tile(j):
         g = dot(rx_t[...], dcat[:, lane(j, 2 * LANES)])
@@ -363,13 +415,7 @@
         squared[1] += squares(g[:, :LANES])
         squared[2] += squares(g[:, LANES:])
 
-    half = tiles // 2
-    every(0, half, grad_tile)
-    every(1, groups, lambda i: across(parcel, pmp, psem, i).wait_recv())
-    psend[...] = total_of(pmp, groups)
-    every(1, n, lambda i: around(psend, pex, pesem, i).start())
-    pex[me] = psend[...]
-    every(half, tiles, grad_tile)
+    every(0, tiles, grad_tile)
     puts = [
         pltpu.make_async_copy(gg, gate_grad, osem.at[0]),
         pltpu.make_async_copy(gu, up_grad, osem.at[1]),
@@ -377,36 +423,46 @@
     ]
     puts[0].start()
     puts[1].start()
-    norms[0:8, :] = squared[1]
-    norms[8:16, :] = squared[2]
-    every(1, groups, lambda i: across(norms, nmp, nsem, i).start())
-    nmp[col] = norms[...]
-    every(1, n, lambda i: around(psend, pex, pesem, i).wait_recv())
-    down_norm = pex[0, n : n + 8, :]
-    for e in range(1, n):
-        down_norm = down_norm + pex[e, n : n + 8, :]
-    inv_down[...] = inverse_rms(down_norm, total_count)
+    parcel[n : n + 8, :] = squared[1]
+    parcel[n + 8 : n + 16, :] = squared[2]
+    every(1, groups, lambda i: across(parcel, pmp, nsem, i).start())
+    every(1, highs, lambda h: lend(h, 1).start())
+    pmp[col] = parcel[...]
+    every(1, n, lambda i: around(dsend, dex, pesem, i).wait_recv())
+    fold_table(
+        units, table, folded, inverse_rms(total_of(dex, n), total_count), float((hidden * groups) ** 0.5)
+    )
 
     strips = width // LANES
     bands = hidden // CHUNK
-    down_scale = float((hidden * groups) ** 0.5)
+
+    def balanced(ref, g, w):
+        value = network(units, ref, units // 2, units - units // 2, g, w)
+        return (value * tall(table[5 * units + 2], g.shape[0])).astype(BF16)
 
     def update_band(lo, hi):
         def body(step):
             r = pl.ds(pl.multiple_of((step // strips) * CHUNK, CHUNK), CHUNK)
             c = lane(lax.rem(step, strips))
-            f0 = gd[r, c] * tall(inv_down[...], CHUNK)
-            dout[r, c] = network(units, table, f0, vd[r, c].astype(F32) * down_scale)
+            dout[r, c] = balanced(folded, gd[r, c], vd[r, c].astype(F32))
 
         every(lo * strips, hi * strips, body)
 
     marks = [i * bands // 7 for i in range(8)]
     update_band(marks[0], marks[1])
 
-    every(1, groups, lambda i: across(norms, nmp, nsem, i).wait_recv())
-    nsend[...] = total_of(nmp, groups)
-    every(1, n, lambda i: around(nsend, nex, nesem, i).start())
-    nex[me] = nsend[...]
+    every(1, groups, lambda i: across(parcel, pmp, nsem, i).wait_recv())
+    psend[...] = total_of(pmp, groups)
+    every(1, n, lambda i: around(psend, pex, nesem, i).start())
+    pex[me] = psend[...]
+
+    update_band(marks[1], marks[3])
+    every(1, n, lambda i: around(psend, pex, nesem, i).wait_recv())
+    both_norms = pex[0, n : n + 16, :]
+    for e in range(1, n):
+        both_norms = both_norms + pex[e, n : n + 16, :]
+    inv_gate[...] = inverse_rms(both_norms[0:8, :], total_count)
+    inv_up[...] = inverse_rms(both_norms[8:16, :], total_count)
 
     g0, g1 = gates[0:1, :], gates[1:2, :]
     gated0 = jnp.zeros((1, toks), F32)
@@ -423,9 +479,8 @@
     every(1, n, lambda i: around(rpart, rex, rsem, i).start())
     rex[me] = rpart[...]
 
-    update_band(marks[1], marks[2])
-
-    every(1, highs, lambda h: lend(h).wait_recv())
+    every(1, highs, lambda h: lend(h, 0).wait_recv())
+    every(1, highs, lambda h: lend(h, 1).wait_recv())
     summed = part[col].astype(F32) + prec[pair].astype(F32)
     for h in range(1, highs):
         summed = summed + hrec[lax.rem(pair + h, highs)].astype(F32)
@@ -439,17 +494,11 @@
     own_r = pltpu.make_async_copy(back.at[rows(me)], ret.at[rows(me)], own.at[2])
     own_r.start()
 
-    update_band(marks[2], marks[4])
+    update_band(marks[3], marks[5])
     every(1, n, lambda i: around(rpart, rex, rsem, i).wait_recv())
     rsum[...] = total_of(rex, n)
     every(1, groups, lambda i: across(rsum, rmp, rmsem, i).start())
     rmp[col] = rsum[...]
-
-    update_band(marks[4], marks[5])
-    every(1, n, lambda i: around(nsend, nex, nesem, i).wait_recv())
-    both_norms = total_of(nex, n)
-    inv_gate[...] = inverse_rms(both_norms[0:8, :], total_count)
-    inv_up[...] = inverse_rms(both_norms[8:16, :], total_count)
 
     update_band(marks[5], marks[6])
     every(1, groups, lambda i: across(rsum, rmp, rmsem, i).wait_recv())
@@ -462,7 +511,7 @@
         for s in range(colw // LANES):
             c = slice(m * colw + s * LANES, m * colw + (s + 1) * LANES)
             f0 = rmp[m, :, s * LANES : (s + 1) * LANES] * tall(router_inv, n)
-            router_out[:, c] = network(units, table, f0, router[:, c].astype(F32) * float(width**0.5))
+            router_out[:, c] = balanced(table, f0, router[:, c].astype(F32) * float(width**0.5))
 
     update_band(marks[6], marks[7])
     puts[2].start()
@@ -477,14 +526,14 @@
     def finish(i):
         spread_x(i).wait_send()
         spread_y(i).wait_send()
-        around(psend, pex, pesem, i).wait_send()
-        around(nsend, nex, nesem, i).wait_send()
+        around(dsend, dex, pesem, i).wait_send()
+        around(psend, pex, nesem, i).wait_send()
         around(rpart, rex, rsem, i).wait_send()
         bring(i).wait_send()
 
     def finish_mp(i):
-        across(parcel, pmp, psem, i).wait_send()
-        across(norms, nmp, nsem, i).wait_send()
+        across(norm_down, dmp, psem, i).wait_send()
+        across(parcel, pmp, nsem, i).wait_send()
         across(rsum, rmp, rmsem, i).wait_send()
 
     every(1, n, finish)
@@ -492,7 +541,8 @@
     every(0, n, sent_x)
     every(0, n, sent_y)
     every(0, highs, lambda q: give(q).wait_send())
-    every(1, highs, lambda h: lend(h).wait_send())
+    every(1, highs, lambda h: lend(h, 0).wait_send())
+    every(1, highs, lambda h: lend(h, 1).wait_send())
     for put in puts:
         put.wait()
 
@@ -516,7 +566,7 @@
     def f(*shape):
         return pltpu.VMEM(shape, F32)
 
-    lines = n + 8
+    lines = n + 16
     up_highs = max(highs - 1, 1)
     return pl.pallas_call(
         functools.partial(step_kernel, n, groups, cap, units, total_count),
@@ -542,12 +592,12 @@
             v(groups, slots, colw), v(highs, slots, colw), v(highs, slots, colw), v(highs, slots, colw),
             v(slots, colw), v(slots, colw),
             f(lines, LANES), f(groups, lines, LANES), f(lines, LANES), f(n, lines, LANES),
-            f(16, LANES), f(groups, 16, LANES), f(16, LANES), f(n, 16, LANES),
+            f(8, LANES), f(groups, 8, LANES), f(8, LANES), f(n, 8, LANES),
             f(n, colw), f(n, n, colw), f(n, colw), f(groups, n, colw),
-            v(hidden, width), f(5 * units + 1, 8, LANES), f(8, LANES), f(3, 8, LANES),
+            v(hidden, width), f(5 * units + 3, 8, LANES), f(5 * units + 3, 8, LANES), f(3, 8, LANES),
             dma((4,)), dma((3,)), dma((3,)), dma((3,)),
             dma((4, n)), dma((4, up_highs, n)), dma((4, n)), dma((4, up_highs, n)),
-            dma((2, highs)), dma((2, highs)), dma((2, n)),
+            dma((2, highs)), dma((2, 2, highs)), dma((2, n)),
             dma((2, groups)), dma((2, n)), dma((2, groups)), dma((2, n)), dma((2, n)), dma((2, groups)),
         ],
         compiler_params=pltpu.CompilerParams(
@@ -579,29 +629,9 @@
     return positive
 
 
-def ordered_network(units, table, sure, g, w):
-    rows = g.shape[0]
-
-    def coef(i):
-        return tall(table[i], rows)
-
-    f2 = jnp.tanh(g * coef(5 * units + 1))
-    acc = coef(5 * units)
-    for j in range(units):
-        y = coef(j) * g + coef(units + j) * w + coef(2 * units + j) * f2
-        part = jnp.maximum(y, coef(3 * units + j))
-        if j < sure:
-            acc = acc + part
-        elif j == sure:
-            acc = acc + coef(4 * units + j) * part
-        else:
-            acc = acc - part
-    return acc.astype(BF16)
-
-
 def update_kernel(
     units, scale, gate_grad, up_grad, gate_hbm, up_hbm, inv_gate, inv_up, mlp_in, mlp_bias, mlp_out,
-    gate_out, up_out, gate_g, up_g, gate_w, up_w, gate_new, up_new, table, gsem, wsem, osem,
+    mixed_in, down_in, router_in, gate_out, up_out, mixed_out, down_out, router_out, mixed, down, router, gate_g, up_g, gate_w, up_w, gate_new, up_new, table, gsem, wsem, osem, psem,
 ):
     width, hidden = gate_grad.shape
     strips = hidden // LANES
@@ -624,6 +654,11 @@
 
     every(0, bands, lambda b: begin(0, b))
     every(0, bands, lambda b: begin(1, b))
+    passing = ((mixed_in, mixed, mixed_out), (down_in, down, down_out), (router_in, router, router_out))
+    taken = [pltpu.make_async_copy(a, b, psem.at[0, k]) for k, (a, b, _) in enumerate(passing)]
+    given = [pltpu.make_async_copy(b, c, psem.at[1, k]) for k, (_, b, c) in enumerate(passing)]
+    for copy in taken:
+        copy.start()
 
     def tensor(k, g_ref, w_ref, inv, new, out):
         positive = ordered_table(units, table, mlp_in, mlp_bias, mlp_out, inv[...], scale)
@@ -641,9 +676,9 @@
                         copy.wait()
 
                     def strip(c):
-                        new[r, lane(c)] = ordered_network(
-                            units, table, sure, g_ref[r, lane(c)], w_ref[r, lane(c)].astype(F32)
-                        )
+                        new[r, lane(c)] = network(
+                            units, table, sure, 1, g_ref[r, lane(c)], w_ref[r, lane(c)].astype(F32)
+                        ).astype(BF16)
 
                     every(0, strips, strip)
                     put(b).start()
@@ -652,15 +687,19 @@
 
         return put
 
-    puts = [
-        tensor(0, gate_g, gate_w, inv_gate, gate_new, gate_out),
-        tensor(1, up_g, up_w, inv_up, up_new, up_out),
-    ]
+    puts = [tensor(0, gate_g, gate_w, inv_gate, gate_new, gate_out)]
+    for copy in taken:
+        copy.wait()
+    for copy in given:
+        copy.start()
+    puts.append(tensor(1, up_g, up_w, inv_up, up_new, up_out))
+    for copy in given:
+        copy.wait()
     for put in puts:
         every(0, bands, lambda b: put(b).wait())
 
 
-def update(gate_grad, up_grad, w_gate, w_up, inv_gate, inv_up, mlp_in, mlp_bias, mlp_out):
+def update(gate_grad, up_grad, w_gate, w_up, inv_gate, inv_up, mlp_in, mlp_bias, mlp_out, *passing):
     units = mlp_bias.shape[0]
     width, hidden = gate_grad.shape
     smem = pl.BlockSpec(memory_space=pltpu.SMEM)
@@ -669,10 +708,10 @@
     shape = jax.ShapeDtypeStruct((width, hidden), BF16)
     return pl.pallas_call(
         functools.partial(update_kernel, units, float(width**0.5)),
-        out_shape=(shape, shape),
-        in_specs=[hbm] * 4 + [vmem] * 2 + [smem] * 3,
-        out_specs=(hbm, hbm),
-        scratch_shapes=[
+        out_shape=(shape, shape) + tuple(jax.ShapeDtypeStruct(x.shape, x.dtype) for x in passing),
+        in_specs=[hbm] * 4 + [vmem] * 2 + [smem] * 3 + [hbm] * 3,
+        out_specs=(hbm,) * 5,
+        scratch_shapes=[pltpu.VMEM(x.shape, x.dtype) for x in passing] + [
             pltpu.VMEM((width, hidden), F32),
             pltpu.VMEM((width, hidden), F32),
             pltpu.VMEM((width, hidden), BF16),
@@ -683,6 +722,7 @@
             pltpu.SemaphoreType.DMA((2, width // CHUNK)),
             pltpu.SemaphoreType.DMA((2, width // CHUNK)),
             pltpu.SemaphoreType.DMA((2, width // CHUNK)),
+            pltpu.SemaphoreType.DMA((2, 3)),
         ],
         compiler_params=pltpu.CompilerParams(vmem_limit_bytes=60 * 1024 * 1024),
         cost_estimate=pl.CostEstimate(
@@ -690,7 +730,7 @@
             transcendentals=2 * width * hidden,
         ),
         name="update",
-    )(gate_grad, up_grad, w_gate, w_up, inv_gate, inv_up, mlp_in, mlp_bias, mlp_out)
+    )(gate_grad, up_grad, w_gate, w_up, inv_gate, inv_up, mlp_in, mlp_bias, mlp_out, *passing)
 
 
 def on_device(
@@ -705,8 +745,9 @@
         tokens, cotangent, routes.T, router_weight.T, w_gate, w_up, w_down,
         mlp_in, mlp_bias, mlp_out, n, groups, total_count,
     )
-    gate_update, up_update = update(
-        gate_grad, up_grad, w_gate, w_up, inv_gate, inv_up, mlp_in, mlp_bias, mlp_out
+    gate_update, up_update, mixed, down_update, router_update = update(
+        gate_grad, up_grad, w_gate, w_up, inv_gate, inv_up, mlp_in, mlp_bias, mlp_out,
+        mixed, down_update, router_update,
     )
     return (mixed, gate_update[None], up_update[None], down_update[None], router_update.T)
 

time: 109 us -> 100 us (0.917)
  Pallas kernels: 106 us -> 99.2 us
  local copies, waits for them, and re-layouts: 2.5 us -> 0 us
    pallas_call x1, Pallas kernels: 72.9 us -> 66.4 us  [fused_step(): pl.pallas_call(functools.partial(step_kernel, n, groups, cap, units, tota...]
    unnamed x9 -> x0, local copies, waits for them, and re-layouts: 2.5 us -> none
where the time goes in v3:
time: 100 us; the launch traced here: 99.8 us
  Pallas kernels  99.2 us (99%)
    pallas_call x1, Pallas kernels, fused_step(): pl.pallas_call(functools.partial(step_kernel, n, groups, cap, units, tota...  66.4 us
    pallas_call x1, Pallas kernels, update(): pl.pallas_call(functools.partial(update_kernel, units, float(width ** 0.5...  32.8 us

profile of v3, /device:TPU:0, one launch (start us, length us, event | category | flops | bytes accessed | tf_op | source)
XLA Modules:
  0.0 99.8 jit_solution(2741718494400895102)
XLA Ops:
  0.6 66.4 %fused_step.1 = (bf16[256,256]{1,0:T(8,128)(2,1)}, bf16[896,1024]{1,0:T(8,128)(2,1)}, bf16[8,1024]{1,0:T(8,128)(2,1)}, f32[8,128]{1,0:T(8,128)}, f32[8,128]{1,0:...) custom-call(bf16[256,1024]{1,0:T(8,128)(2,1)} %tokens_hbm.1, bf16[256,1024]{1,0:T(8,128)(2,1)} %cot_hbm.1, ...), custom_call_target="tpu_custom_call" | custom-call | tf_op jit(solution)/shard_map/fused_step/pallas_call | solution.py:571
  67.1 32.8 %update.1 = (bf16[1024,896]{1,0:T(8,128)(2,1)}, bf16[1024,896]{1,0:T(8,128)(2,1)}, bf16[256,256]{1,0:T(8,128)(2,1)}, bf16[896,1024]{1,0:T(8,128)(2,1)}, bf16[8,1024]{1,0:T(8,128)(2,1)}) custom-call(f32[1024,896]{1,0:T(8,128)} %get-tuple-element.17.gate_grad, f32[1024,896]{1,0:T(8,128)} %get-tuple-element.18.up_grad, bf16[1024,896]{1,0:T(8,128)(2,1)} %bitcast.10, ...), custom_call_target="tpu_custom_call" | custom-call | flops 264241152 | bytes 3670016 | tf_op jit(solution)/shard_map/update/pallas_call | solution.py:709
